TPU v7x, 32 devices: a whole 2x2x4 slice. The times are simulated.
32 devices in a mesh: gx: 8 (over z, x), gy: 4 (over y, core).
Axes of the slice: x: 2, y: 2, z: 4, core: 2. Of those that a mesh axis runs over, the one named last changes fastest.
Arguments:
- rhs: float32 [128, 128, 128], P('gx', 'gy'), may hold values from -6 to 6
- target: float32 [128, 128, 128], P('gx', 'gy'), may hold values from -6 to 6
- stencils: float32 [9, 27], replicated, may hold values from -0.006 to 0.11, as said below
- face_mask: int32 [6], replicated, may hold values 0 or 1
Outputs:
- solution: float32 [128, 128, 128], P('gx', 'gy')
- grad_rhs: float32 [128, 128, 128], P('gx', 'gy')
- grad_stencils: float32 [9, 27], replicated
Inputs may be any that keep to these rules, and one draw needn't show every extreme that they name: `stencils`: entry 13 of every row lies in 0.05 to 0.11, entries 4, 10, 12, 14, 16, 22 in 0.005 to 0.02, the others in -0.006 to 0.006.
All inputs are finite; a program needn't handle non-finite values.
Results may differ from a plain program's by a relative error of at most 0.00002.
Values sent between devices are 32-bit elements; how exact they have to be, the bound alone decides.
No kernel may reach another device: no remote copies, remote signals or barrier semaphores. Data moves between devices by JAX's collectives and lax.ppermute only.
A program may use at most 128 MiB of HBM per device.

v0:
```python
import jax
import jax.numpy as jnp
from jax import lax
from jax.sharding import PartitionSpec as P

LEVELS = 4
SWEEPS = 3


def extended(array, sides, width):
    for axis, dim in sides:
        peers, length = (lax.axis_size(axis), array.shape[dim])
        up = [(i, (i + 1) % peers) for i in range(peers - 1)]
        down = [(j, i) for i, j in up]
        last = lax.slice_in_dim(array, length - width, length, axis=dim)
        initial = lax.slice_in_dim(array, 0, width, axis=dim)
        before = lax.ppermute(last, axis, up)
        after = lax.ppermute(initial, axis, down)
        array = jnp.concatenate([before, array, after], axis=dim)
    return array


def shifted_sum(padded, weights, shape):
    total = jnp.zeros(shape, jnp.float32)
    for shift_first in range(3):
        for shift_second in range(3):
            for shift_third in range(3):
                window = padded[
                    shift_first : shift_first + shape[0],
                    shift_second : shift_second + shape[1],
                    shift_third : shift_third + shape[2],
                ]
                total = total + weights[9 * shift_first + 3 * shift_second + shift_third] * window
    return total


def weight_sums(cotangent, padded):
    shape = cotangent.shape
    sums = []
    for shift_first in range(3):
        for shift_second in range(3):
            for shift_third in range(3):
                window = padded[
                    shift_first : shift_first + shape[0],
                    shift_second : shift_second + shape[1],
                    shift_third : shift_third + shape[2],
                ]
                sums.append(jnp.sum(cotangent * window))
    return jnp.stack(sums)


def operate(padded, field, tally):
    beside = padded[2:, 1:-1, 1:-1] + padded[:-2, 1:-1, 1:-1]
    beside = beside + padded[1:-1, 2:, 1:-1] + padded[1:-1, :-2, 1:-1]
    beside = beside + padded[1:-1, 1:-1, 2:] + padded[1:-1, 1:-1, :-2]
    return (6.0 - tally) * field - beside


def restrict(field):
    shape = field.shape
    return field.reshape(shape[0] // 2, 2, shape[1] // 2, 2, shape[2]).mean(axis=(1, 3))


def prolong(field):
    return jnp.repeat(jnp.repeat(field, 2, axis=0), 2, axis=1)


def block_sums(field):
    shape = field.shape
    return field.reshape(shape[0] // 2, 2, shape[1] // 2, 2, shape[2]).sum(axis=(1, 3))


def face_tally(shape, start_first, start_second, total_first, total_second, face_mask):
    walls = face_mask.astype(jnp.float32)
    first = start_first + lax.broadcasted_iota(jnp.int32, shape, 0)
    second = start_second + lax.broadcasted_iota(jnp.int32, shape, 1)
    third = lax.broadcasted_iota(jnp.int32, shape, 2)
    tally = walls[0] * (first == 0).astype(jnp.float32) + walls[1] * (
        first == total_first - 1
    ).astype(jnp.float32)
    tally = (
        tally
        + walls[2] * (second == 0).astype(jnp.float32)
        + walls[3] * (second == total_second - 1).astype(jnp.float32)
    )
    tally = (
        tally
        + walls[4] * (third == 0).astype(jnp.float32)
        + walls[5] * (third == shape[2] - 1).astype(jnp.float32)
    )
    return tally


def level_tally(shape, face_mask):
    start_first = lax.axis_index("gx") * shape[0]
    start_second = lax.axis_index("gy") * shape[1]
    return face_tally(
        shape,
        start_first,
        start_second,
        shape[0] * lax.axis_size("gx"),
        shape[1] * lax.axis_size("gy"),
        face_mask,
    )


def loop_tally(shape, face_mask):
    start_first = lax.axis_index("gx") * shape[0] - 1
    start_second = lax.axis_index("gy") * shape[1] - 1
    wider = (shape[0] + 2, shape[1] + 2, shape[2])
    return face_tally(
        wider,
        start_first,
        start_second,
        shape[0] * lax.axis_size("gx"),
        shape[1] * lax.axis_size("gy"),
        face_mask,
    )


def loop_inside(shape):
    wider = (shape[0] + 2, shape[1] + 2, shape[2])
    first = lax.axis_index("gx") * shape[0] - 1 + lax.broadcasted_iota(jnp.int32, wider, 0)
    second = lax.axis_index("gy") * shape[1] - 1 + lax.broadcasted_iota(jnp.int32, wider, 1)
    inside = (
        (first >= 0)
        & (first < shape[0] * lax.axis_size("gx"))
        & (second >= 0)
        & (second < shape[1] * lax.axis_size("gy"))
    )
    return inside.astype(jnp.float32)


def coarse_tally(shape, face_mask):
    start_second = lax.axis_index("gy") * shape[1]
    return face_tally(shape, 0, start_second, shape[0], shape[1] * lax.axis_size("gy"), face_mask)


def widen_level(field):
    rimmed = extended(field, (("gx", 0), ("gy", 1)), 1)
    return jnp.pad(rimmed, ((0, 0), (0, 0), (1, 1)))


def widen_deep(field):
    rimmed = extended(field, (("gx", 0), ("gy", 1)), 2)
    return jnp.pad(rimmed, ((0, 0), (0, 0), (1, 1)))


def smooth_then_apply(field, weights, tally):
    shape = field.shape
    deep = widen_deep(field)
    wider = (shape[0] + 2, shape[1] + 2, shape[2])
    smoothed_loop = shifted_sum(deep, weights, wider) * loop_inside(shape)
    smoothed = smoothed_loop[1:-1, 1:-1]
    applied = operate(jnp.pad(smoothed_loop, ((0, 0), (0, 0), (1, 1))), smoothed, tally)
    return (smoothed, applied, deep[1:-1, 1:-1])


def apply_then_smooth(middle, source_wide, weights, face_mask):
    shape = middle.shape
    deep = widen_deep(middle)
    source_loop = source_wide[:, :, 1:-1]
    applied_loop = operate(deep, deep[1:-1, 1:-1, 1:-1], loop_tally(shape, face_mask))
    after_loop = (source_loop - applied_loop) * loop_inside(shape)
    after_wide = jnp.pad(after_loop, ((0, 0), (0, 0), (1, 1)))
    after = after_loop[1:-1, 1:-1]
    smoothed = shifted_sum(after_wide, weights, shape)
    return (after, after_wide, smoothed)


def widen_coarse(field):
    rimmed = extended(field, (("gy", 1),), 1)
    return jnp.pad(rimmed, ((1, 1), (0, 0), (1, 1)))


def agglomerate(field):
    return lax.all_gather(field, "gx", axis=0, tiled=True)


def own_block(whole, shape):
    start_first = lax.axis_index("gx") * shape[0]
    block = lax.dynamic_slice_in_dim(whole, start_first, shape[0], 0)
    return block


def coarse_owner():
    return jnp.where(lax.axis_index("gx") == 0, 1.0, 0.0).astype(jnp.float32)


def on_device(rhs, target, stencils, face_mask):
    saved = []
    source = rhs
    for height in range(LEVELS):
        tally = level_tally(source.shape, face_mask)
        presmooth, applied, source_wide = smooth_then_apply(source, stencils[height], tally)
        remainder = source - applied
        saved.append((source, source_wide, presmooth, tally))
        source = restrict(remainder)
    coarse_shape = source.shape
    whole_source = agglomerate(source)
    whole_shape = whole_source.shape
    whole_tally = coarse_tally(whole_shape, face_mask)
    coarse_weights = stencils[2 * LEVELS]
    inputs = [widen_coarse(whole_source)]
    iterate = shifted_sum(inputs[0], coarse_weights, whole_shape)
    for sweep_index in range(SWEEPS - 1):
        remainder = whole_source - operate(widen_coarse(iterate), iterate, whole_tally)
        inputs.append(widen_coarse(remainder))
        iterate = iterate + shifted_sum(inputs[-1], coarse_weights, whole_shape)
    correction = own_block(iterate, coarse_shape)
    posts = [None] * LEVELS
    for height in reversed(range(LEVELS)):
        source, source_wide, presmooth, tally = saved[height]
        middle = presmooth + prolong(correction)
        after, after_wide, smoothed = apply_then_smooth(
            middle, source_wide, stencils[LEVELS + height], face_mask
        )
        correction = middle + smoothed
        posts[height] = (after, after_wide)
    error = correction - target
    grads = [None] * (2 * LEVELS + 1)
    upward = []
    cotangent = error
    for height in range(LEVELS):
        source, source_wide, presmooth, tally = saved[height]
        after, after_wide = posts[height]
        grads[LEVELS + height] = weight_sums(cotangent, after_wide)
        grad_after, applied, unused = smooth_then_apply(
            cotangent, stencils[LEVELS + height][::-1], tally
        )
        grad_middle = cotangent - applied
        upward.append((grad_after, grad_middle))
        cotangent = block_sums(grad_middle)
    grad_iterate = agglomerate(cotangent)
    flipped = coarse_weights[::-1]
    grad_source = jnp.zeros(whole_shape, jnp.float32)
    coarse_grad = jnp.zeros((27,), jnp.float32)
    for sweep_index in reversed(range(SWEEPS - 1)):
        coarse_grad = coarse_grad + weight_sums(grad_iterate, inputs[sweep_index + 1])
        grad_remainder = shifted_sum(widen_coarse(grad_iterate), flipped, whole_shape)
        grad_source = grad_source + grad_remainder
        grad_iterate = grad_iterate - operate(
            widen_coarse(grad_remainder), grad_remainder, whole_tally
        )
    coarse_grad = coarse_grad + weight_sums(grad_iterate, inputs[0])
    grad_source = grad_source + shifted_sum(widen_coarse(grad_iterate), flipped, whole_shape)
    grads[2 * LEVELS] = coarse_grad * coarse_owner()
    grad_down = own_block(grad_source, coarse_shape)
    for height in reversed(range(LEVELS)):
        source, source_wide, presmooth, tally = saved[height]
        grad_after, grad_middle = upward[height]
        grad_remainder = 0.25 * prolong(grad_down)
        grad_level = grad_after + grad_remainder
        grad_pre = grad_middle - operate(widen_level(grad_remainder), grad_remainder, tally)
        grads[height] = weight_sums(grad_pre, source_wide)
        grad_level = grad_level + shifted_sum(
            widen_level(grad_pre), stencils[height][::-1], source.shape
        )
        grad_down = grad_level
    totals = lax.psum(jnp.stack(grads), ("gx", "gy"))
    cells_total = (
        rhs.shape[0] * lax.axis_size("gx") * rhs.shape[1] * lax.axis_size("gy") * rhs.shape[2]
    )
    return (correction, grad_down, totals / cells_total)


def solution(mesh):
    placed = (P("gx", "gy", None), P("gx", "gy", None), P(), P())
    return jax.shard_map(
        on_device,
        mesh=mesh,
        in_specs=placed,
        out_specs=(P("gx", "gy", None), P("gx", "gy", None), P()),
        check_vma=False,
    )
```

profile of v0, /device:TPU:0, one launch (start us, length us, event | category | flops | bytes accessed | tf_op | source)
XLA Modules:
  0.0 1091.2 jit_solution(3935114857322131630)
XLA Ops:
  2.8 5.5 collective-permute-start
  41.6 19.2 %fusion.109 = f32[18,34,128]{2,1,0:T(8,128)S(1)} fusion(f32[20,36,128]{2,1,0:T(8,128)S(1)} %pad_maximum_fusion, f32[20,2,128]{2,1,0:T(2,128)S(1)} %collective-permute-done.3, f32[20,32,128]{2,1,0:T(8,128)S(1)} %constant_dynamic-update-slice_fusion, f32[20,2,128]{2,1,0:T(2,128)S(1)} %collective-permute-done.2, f32[]{:T(128)} %bitcast.26, f32[]{:T(128)} %bitcast.25, ...), kind=kLoop, calls=%fused_computation.426 | loop fusion | flops 4856832 | bytes 2198654 | tf_op jit(solution)/shard_map/mul | solution.py:153
  61.9 4.3 collective-permute-start.4
  79.0 18.0 %fusion.299 = f32[10,18,128]{2,1,0:T(8,128)S(1)} fusion(f32[12,20,128]{2,1,0:T(8,128)S(1)} %pad_maximum_fusion.25, f32[12,18,128]{2,1,0:T(8,128)S(1)} %get-tuple-element.371, f32[12,18,128]{2,1,0:T(8,128)S(1)} %get-tuple-element.370, f32[]{:T(128)} %bitcast.60, f32[]{:T(128)} %bitcast.59, f32[]{:T(128)} %bitcast.58, f32[]{:T(128)} %bitcast.57, f32[]{:T(128)} %bitcast.56, ...), kind=kLoop, calls=%fused_computation.754 | loop fusion | flops 1290240 | bytes 1346192 | tf_op jit(solution)/shard_map/mul | solution.py:153
  113.3 17.7 %fusion.486 = f32[6,10,128]{2,1,0:T(8,128)S(1)} fusion(f32[8,12,128]{2,1,0:T(8,128)S(1)} %pad_maximum_fusion.49, f32[8,10,128]{2,1,0:T(8,128)S(1)} %get-tuple-element.407, f32[8,10,128]{2,1,0:T(8,128)S(1)} %get-tuple-element.406, f32[]{:T(128)} %bitcast.88, f32[]{:T(128)} %bitcast.87, f32[]{:T(128)} %bitcast.86, f32[]{:T(128)} %bitcast.85, f32[]{:T(128)} %bitcast.84, ...), kind=kLoop, calls=%fused_computation.1075 | loop fusion | flops 430080 | bytes 539264 | tf_op jit(solution)/shard_map/mul | solution.py:153
  132.4 4.9 collective-permute-start.12
  138.7 4.0 collective-permute-start.14
  146.5 17.7 %fusion.595 = f32[4,6,128]{2,1,0:T(8,128)S(1)} fusion(f32[6,8,128]{2,1,0:T(8,128)S(1)} %pad_maximum_fusion.61, f32[6,6,128]{2,1,0:T(8,128)S(1)} %get-tuple-element.431, f32[6,6,128]{2,1,0:T(8,128)S(1)} %get-tuple-element.430, f32[]{:T(128)} %bitcast.116, f32[]{:T(128)} %bitcast.115, f32[]{:T(128)} %bitcast.114, f32[]{:T(128)} %bitcast.113, f32[]{:T(128)} %bitcast.112, ...), kind=kLoop, calls=%fused_computation.1260 | loop fusion | flops 172032 | bytes 184952 | tf_op jit(solution)/shard_map/mul | solution.py:153
  164.3 19.8 %all-gather.2 = f32[8,2,128]{2,1,0:T(2,128)S(1)} all-gather(f32[1,2,128]{2,1,0:T(2,128)S(1)} %multiply_bitcast_fusion), channel_id=2, replica_groups=mesh['gx'=8,'gy'=4] {'gx'}, dimensions={0}, use_global_device_ids=true | all-gather | bytes 9216 | tf_op jit(solution)/shard_map/all_gather | solution.py:177
  191.6 16.7 %multiply_add_fusion.1 = f32[8,2,128]{2,1,0:T(2,128)S(1)} fusion(f32[8,2,128]{2,1,0:T(2,128)S(1)} %all-gather.2, f32[10,4,130]{2,1,0:T(4,128)S(1)} %select_maximum_fusion.42, f32[]{:T(128)} %bitcast.145, f32[]{:T(128)} %bitcast.144, f32[]{:T(128)} %bitcast.143, f32[]{:T(128)} %bitcast.142, f32[]{:T(128)} %bitcast.141, f32[]{:T(128)} %bitcast.140, ...), kind=kLoop, calls=%fused_computation.1766 | loop fusion | flops 112640 | bytes 221292 | tf_op jit(solution)/shard_map/add | solution.py:33
  208.3 4.3 collective-permute-start.18
  216.1 4.3 collective-permute-start.20
  224.0 16.7 %add_add_fusion.3 = f32[8,2,128]{2,1,0:T(2,128)S(1)} fusion(f32[8,2,128]{2,1,0:T(2,128)S(1)} %multiply_add_fusion.1, f32[8,2,128]{2,1,0:T(2,128)S(1)} %fusion.775, f32[10,4,130]{2,1,0:T(4,128)S(1)} %select_maximum_fusion.38, f32[]{:T(128)} %bitcast.145, f32[]{:T(128)} %bitcast.144, f32[]{:T(128)} %bitcast.143, f32[]{:T(128)} %bitcast.142, f32[]{:T(128)} %bitcast.141, ...), kind=kLoop, calls=%fused_computation.1764 | loop fusion | flops 114688 | bytes 229484 | tf_op jit(solution)/shard_map/add | solution.py:209
  255.6 13.7 %multiply_add_fusion = f32[8,2,128]{2,1,0:T(2,128)S(1)} fusion(f32[8,2,128]{2,1,0:T(2,128)S(1)} %fusion.771, f32[10,4,130]{2,1,0:T(4,128)S(1)} %select_maximum_fusion.34, f32[]{:T(128)} %bitcast.140, f32[]{:T(128)} %bitcast.139, f32[]{:T(128)} %bitcast.138, f32[]{:T(128)} %bitcast.137, f32[]{:T(128)} %bitcast.136, f32[]{:T(128)} %bitcast.135, ...), kind=kLoop, calls=%fused_computation.1763 | loop fusion | flops 92160 | bytes 180312 | tf_op jit(solution)/shard_map/add | solution.py:33
  273.0 4.5 collective-permute-start.26
  286.1 17.1 %add_add_fusion.4 = f32[2,4,128]{2,1,0:T(4,128)S(1)} fusion(f32[4,6,128]{2,1,0:T(8,128)S(1)} %fusion.501, f32[]{:T(128)} %bitcast.174, f32[]{:T(128)} %bitcast.173, f32[]{:T(128)} %bitcast.172, f32[]{:T(128)} %bitcast.171, f32[]{:T(128)} %bitcast.170, f32[]{:T(128)} %bitcast.169, f32[]{:T(128)} %bitcast.168, f32[]{:T(128)} %bitcast.167, f32[]{:T(128)} %bitcast.166, ...), kind=kLoop, calls=%fused_computation.1933 | loop fusion | flops 56320 | bytes 63596 | tf_op jit(solution)/shard_map/add | solution.py:218
  303.3 4.1 collective-permute-start.30
  320.7 16.8 %add_add_fusion.2 = f32[4,8,128]{2,1,0:T(8,128)S(1)} fusion(f32[4,8,128]{2,1,0:T(8,128)S(1)} %slice_add_fusion.30, f32[6,10,128]{2,1,0:T(8,128)S(1)} %fusion.400, f32[]{:T(128)} %bitcast.203, f32[]{:T(128)} %bitcast.202, f32[]{:T(128)} %bitcast.201, f32[]{:T(128)} %bitcast.200, f32[]{:T(128)} %bitcast.199, f32[]{:T(128)} %bitcast.198, f32[]{:T(128)} %bitcast.197, ...), kind=kLoop, calls=%fused_computation.1433 | loop fusion | flops 221184 | bytes 229484 | tf_op jit(solution)/shard_map/add | solution.py:218
  337.6 4.8 collective-permute-start.34
  355.8 17.3 %add_add_fusion.1 = f32[8,16,128]{2,1,0:T(8,128)S(1)} fusion(f32[8,16,128]{2,1,0:T(8,128)S(1)} %slice_add_fusion.19, f32[10,18,128]{2,1,0:T(8,128)S(1)} %fusion.213, f32[]{:T(128)} %bitcast.232, f32[]{:T(128)} %bitcast.231, f32[]{:T(128)} %bitcast.230, f32[]{:T(128)} %bitcast.229, f32[]{:T(128)} %bitcast.228, f32[]{:T(128)} %bitcast.227, f32[]{:T(128)} %bitcast.226, ...), kind=kLoop, calls=%fused_computation.976 | loop fusion | flops 884736 | bytes 843884 | tf_op jit(solution)/shard_map/add | solution.py:218
  390.3 20.5 %multiply_reduce_fusion = (f32[]{:T(128)}, f32[]{:T(128)}, f32[]{:T(128)}, f32[]{:T(128)}, f32[]{:T(128)}, /*index=5*/f32[]{:T(128)}, f32[]{:T(128)}, f32[]{:T(1...) fusion(f32[18,34,128]{2,1,0:T(8,128)S(1)} %fusion.43, ...), kind=kLoop, calls=%fused_computation.577 | loop fusion | flops 5963758 | bytes 3776692 | tf_op jit(solution)/shard_map/reduce_sum | solution.py:48
  415.2 4.2 collective-permute-done.43
  426.6 19.3 %fusion.86 = f32[18,34,128]{2,1,0:T(8,128)S(1)} fusion(f32[20,36,128]{2,1,0:T(8,128)S(1)} %pad_maximum_fusion.2, f32[20,34,128]{2,1,0:T(8,128)S(1)} %get-tuple-element.341, f32[20,34,128]{2,1,0:T(8,128)S(1)} %get-tuple-element.340, f32[]{:T(128)} %bitcast.235, f32[]{:T(128)} %bitcast.236, f32[]{:T(128)} %bitcast.237, f32[]{:T(128)} %bitcast.238, ...), kind=kLoop, calls=%fused_computation.379 | loop fusion | flops 4386816 | bytes 4041854 | tf_op jit(solution)/shard_map/mul | solution.py:153
  451.3 4.2 collective-permute-done.47
  463.2 18.2 %fusion.255 = f32[10,18,128]{2,1,0:T(8,128)S(1)} fusion(f32[12,20,128]{2,1,0:T(8,128)S(1)} %pad_maximum_fusion.28, f32[12,18,128]{2,1,0:T(8,128)S(1)} %get-tuple-element.365, f32[12,18,128]{2,1,0:T(8,128)S(1)} %get-tuple-element.364, f32[]{:T(128)} %bitcast.206, f32[]{:T(128)} %bitcast.207, f32[]{:T(128)} %bitcast.208, f32[]{:T(128)} %bitcast.209, ...), kind=kLoop, calls=%fused_computation.710 | loop fusion | flops 1290240 | bytes 1346192 | tf_op jit(solution)/shard_map/mul | solution.py:153
  483.2 4.6 collective-permute-start.50
  489.1 4.2 collective-permute-done.51
  501.0 17.6 %fusion.442 = f32[6,10,128]{2,1,0:T(8,128)S(1)} fusion(f32[8,12,128]{2,1,0:T(8,128)S(1)} %pad_maximum_fusion.52, f32[8,10,128]{2,1,0:T(8,128)S(1)} %get-tuple-element.401, f32[8,10,128]{2,1,0:T(8,128)S(1)} %get-tuple-element.400, f32[]{:T(128)} %bitcast.177, f32[]{:T(128)} %bitcast.178, f32[]{:T(128)} %bitcast.179, f32[]{:T(128)} %bitcast.180, ...), kind=kLoop, calls=%fused_computation.1031 | loop fusion | flops 430080 | bytes 539264 | tf_op jit(solution)/shard_map/mul | solution.py:153
  522.0 4.5 collective-permute-start.54
  536.3 17.8 %fusion.551 = f32[4,6,128]{2,1,0:T(8,128)S(1)} fusion(f32[6,8,128]{2,1,0:T(8,128)S(1)} %pad_maximum_fusion.64, f32[6,6,128]{2,1,0:T(8,128)S(1)} %get-tuple-element.425, f32[6,6,128]{2,1,0:T(8,128)S(1)} %get-tuple-element.424, f32[]{:T(128)} %bitcast.148, f32[]{:T(128)} %bitcast.149, f32[]{:T(128)} %bitcast.150, f32[]{:T(128)} %bitcast.151, f32[]{:T(128)} %bitcast.152, ...), kind=kLoop, calls=%fused_computation.1216 | loop fusion | flops 172032 | bytes 184952 | tf_op jit(solution)/shard_map/mul | solution.py:153
  557.3 18.6 %all-gather.3 = f32[8,2,128]{2,1,0:T(2,128)S(1)} all-gather(f32[1,2,128]{2,1,0:T(2,128)S(1)} %bitcast.644), channel_id=3, replica_groups=mesh['gx'=8,'gy'=4] {'gx'}, dimensions={0}, use_global_device_ids=true | all-gather | bytes 9216 | tf_op jit(solution)/shard_map/all_gather | solution.py:177
  578.5 4.3 collective-permute-done.59
  582.9 16.7 %fusion.742 = f32[8,2,128]{2,1,0:T(2,128)S(1)} fusion(f32[10,4,130]{2,1,0:T(4,128)S(1)} %select_maximum_fusion.32, f32[8,1,128]{2,1,0:T(1,128)S(1)} %collective-permute-done.59, f32[8,2,128]{2,1,0:T(2,128)S(1)} %all-gather.3, f32[8,1,128]{2,1,0:T(1,128)S(1)} %collective-permute-done.58, f32[]{:T(128)} %bitcast.145, f32[]{:T(128)} %bitcast.144, ...), kind=kLoop, calls=%fused_computation.1593 | loop fusion | flops 112640 | bytes 221292 | tf_op jit(solution)/shard_map/add | solution.py:33
  600.8 4.8 collective-permute-start.60
  618.6 17.0 %stack.1095 = f32[27]{0:T(128)S(1)} concatenate(f32[1]{0:T(128)} %bitcast.400, f32[1]{0:T(128)} %bitcast.401, f32[1]{0:T(128)} %bitcast.402, f32[1]{0:T(128)} %bitcast.403, f32[1]{0:T(128)} %bitcast.404, f32[1]{0:T(128)} %bitcast.405, f32[1]{0:T(128)} %bitcast.406, f32[1]{0:T(128)} %bitcast.407, f32[1]{0:T(128)} %bitcast.408, f32[1]{0:T(128)} %bitcast.409, f32[1]{0:T(128)} %bitcast.410, ...), dimensions={0} | concatenate | bytes 216 | tf_op jit(solution)/shard_map/stack | solution.py:49
  636.5 17.4 %fusion.710 = f32[8,2,128]{2,1,0:T(2,128)S(1)} fusion(f32[10,4,130]{2,1,0:T(4,128)S(1)} %select_maximum_fusion.28, f32[8,1,128]{2,1,0:T(1,128)} %collective-permute-done.63, f32[8,2,128]{2,1,0:T(2,128)S(1)} %copy-done.15, f32[8,1,128]{2,1,0:T(1,128)} %collective-permute-done.62, f32[]{:T(128)} %bitcast.145, f32[]{:T(128)} %bitcast.144, f32[]{:T(128)} %bitcast.143, ...), kind=kLoop, calls=%fused_computation.1530 | loop fusion | flops 112640 | bytes 221292 | tf_op jit(solution)/shard_map/add | solution.py:33
  661.2 4.3 collective-permute-start.66
  669.4 13.5 %fusion.683 = f32[8,2,128]{2,1,0:T(2,128)S(1)} fusion(f32[10,4,130]{2,1,0:T(4,128)S(1)} %select_maximum_fusion.24, f32[8,1,128]{2,1,0:T(1,128)S(1)} %collective-permute-done.67, f32[8,2,128]{2,1,0:T(2,128)S(1)} %get-tuple-element.331, f32[8,1,128]{2,1,0:T(1,128)S(1)} %collective-permute-done.66, f32[]{:T(128)} %bitcast.145, f32[]{:T(128)} %bitcast.144, ...), kind=kLoop, calls=%fused_computation.1477 | loop fusion | flops 92160 | bytes 180312 | tf_op jit(solution)/shard_map/add | solution.py:33
  689.3 16.9 %stack.1124 = f32[27]{0:T(128)S(1)} concatenate(f32[1]{0:T(128)} %bitcast.428, f32[1]{0:T(128)} %bitcast.429, f32[1]{0:T(128)} %bitcast.430, f32[1]{0:T(128)} %bitcast.431, f32[1]{0:T(128)} %bitcast.432, f32[1]{0:T(128)} %bitcast.433, f32[1]{0:T(128)} %bitcast.434, f32[1]{0:T(128)} %bitcast.435, f32[1]{0:T(128)} %bitcast.436, f32[1]{0:T(128)} %bitcast.437, f32[1]{0:T(128)} %bitcast.438, ...), dimensions={0} | concatenate | bytes 216 | tf_op jit(solution)/shard_map/stack | solution.py:49
  714.5 4.4 collective-permute-start.72
  728.5 16.8 %stack.1153 = f32[27]{0:T(128)S(1)} concatenate(f32[1]{0:T(128)} %bitcast.456, f32[1]{0:T(128)} %bitcast.457, f32[1]{0:T(128)} %bitcast.458, f32[1]{0:T(128)} %bitcast.459, f32[1]{0:T(128)} %bitcast.460, f32[1]{0:T(128)} %bitcast.461, f32[1]{0:T(128)} %bitcast.462, f32[1]{0:T(128)} %bitcast.463, f32[1]{0:T(128)} %bitcast.464, f32[1]{0:T(128)} %bitcast.465, f32[1]{0:T(128)} %bitcast.466, ...), dimensions={0} | concatenate | bytes 216 | tf_op jit(solution)/shard_map/stack | solution.py:49
  745.4 17.7 %fusion.816 = f32[2,4,128]{2,1,0:T(4,128)S(1)} fusion(f32[4,6,130]{2,1,0:T(8,128)S(1)} %select_maximum_fusion.44, f32[4,1,128]{2,1,0:T(1,128)S(1)} %collective-permute-done.75, f32[1,4,128]{2,1,0:T(4,128)S(1)} %collective-permute-done.73, f32[2,4,128]{2,1,0:T(4,128)S(1)} %get-tuple-element.334, f32[1,4,128]{2,1,0:T(4,128)S(1)} %collective-permute-done.72, ...), kind=kLoop, calls=%fused_computation.1824 | loop fusion | flops 77824 | bytes 96364 | tf_op jit(solution)/shard_map/mul | solution.py:252
  764.4 4.6 collective-permute-start.77
  775.7 16.9 %stack.1182 = f32[27]{0:T(128)S(1)} concatenate(f32[1]{0:T(128)} %bitcast.484, f32[1]{0:T(128)} %bitcast.485, f32[1]{0:T(128)} %bitcast.486, f32[1]{0:T(128)} %bitcast.487, f32[1]{0:T(128)} %bitcast.488, f32[1]{0:T(128)} %bitcast.489, f32[1]{0:T(128)} %bitcast.490, f32[1]{0:T(128)} %bitcast.491, f32[1]{0:T(128)} %bitcast.492, f32[1]{0:T(128)} %bitcast.493, f32[1]{0:T(128)} %bitcast.494, ...), dimensions={0} | concatenate | bytes 216 | tf_op jit(solution)/shard_map/stack | solution.py:49
  794.2 4.5 collective-permute-start.80
  800.9 4.1 collective-permute-done.81
  805.0 4.6 collective-permute-start.82
  811.7 16.9 %stack.1211 = f32[1,27]{1,0:T(1,128)S(1)} concatenate(f32[1,1]{1,0:T(1,128)} %bitcast.512, f32[1,1]{1,0:T(1,128)} %bitcast.513, f32[1,1]{1,0:T(1,128)} %bitcast.514, f32[1,1]{1,0:T(1,128)} %bitcast.515, f32[1,1]{1,0:T(1,128)} %bitcast.516, f32[1,1]{1,0:T(1,128)} %bitcast.517, f32[1,1]{1,0:T(1,128)} %bitcast.518, f32[1,1]{1,0:T(1,128)} %bitcast.519, f32[1,1]{1,0:T(1,128)} %bitcast.520, ...), dimensions={1} | concatenate | bytes 216 | tf_op jit(solution)/shard_map/stack | solution.py:49
  828.7 17.6 %fusion.628 = f32[4,8,128]{2,1,0:T(8,128)S(1)} fusion(f32[6,10,130]{2,1,0:T(8,128)S(1)} %select_maximum_fusion.16, f32[6,9,128]{2,1,0:T(8,128)S(1)} %get-tuple-element.411, f32[1,8,128]{2,1,0:T(8,128)S(1)} %collective-permute-done.81, f32[4,8,128]{2,1,0:T(8,128)S(1)} %get-tuple-element.335, f32[6,9,128]{2,1,0:T(8,128)S(1)} %get-tuple-element.410, ...), kind=kLoop, calls=%fused_computation.1302 | loop fusion | flops 237568 | bytes 467052 | tf_op jit(solution)/shard_map/mul | solution.py:252
  847.7 5.2 collective-permute-start.85
  853.7 17.1 %stack.1239 = f32[1,27]{1,0:T(1,128)S(1)} concatenate(f32[1,1]{1,0:T(1,128)} %bitcast.539, f32[1,1]{1,0:T(1,128)} %bitcast.540, f32[1,1]{1,0:T(1,128)} %bitcast.541, f32[1,1]{1,0:T(1,128)} %bitcast.542, f32[1,1]{1,0:T(1,128)} %bitcast.543, f32[1,1]{1,0:T(1,128)} %bitcast.544, f32[1,1]{1,0:T(1,128)} %bitcast.545, f32[1,1]{1,0:T(1,128)} %bitcast.546, f32[1,1]{1,0:T(1,128)} %bitcast.547, ...), dimensions={1} | concatenate | bytes 216 | tf_op jit(solution)/shard_map/stack | solution.py:49
  870.8 5.4 collective-permute-start.87
  878.4 17.0 %stack.1267 = f32[1,27]{1,0:T(1,128)S(1)} concatenate(f32[1,1]{1,0:T(1,128)} %bitcast.566, f32[1,1]{1,0:T(1,128)} %bitcast.567, f32[1,1]{1,0:T(1,128)} %bitcast.568, f32[1,1]{1,0:T(1,128)} %bitcast.569, f32[1,1]{1,0:T(1,128)} %bitcast.570, f32[1,1]{1,0:T(1,128)} %bitcast.571, f32[1,1]{1,0:T(1,128)} %bitcast.572, f32[1,1]{1,0:T(1,128)} %bitcast.573, f32[1,1]{1,0:T(1,128)} %bitcast.574, ...), dimensions={1} | concatenate | bytes 216 | tf_op jit(solution)/shard_map/stack | solution.py:49
  897.1 4.5 collective-permute-start.88
  903.0 4.2 collective-permute-done.89
  912.8 17.0 %stack.1066 = f32[27]{0:T(128)S(1)} concatenate(f32[1]{0:T(128)} %bitcast.372, f32[1]{0:T(128)} %bitcast.373, f32[1]{0:T(128)} %bitcast.374, f32[1]{0:T(128)} %bitcast.375, f32[1]{0:T(128)} %bitcast.376, f32[1]{0:T(128)} %bitcast.377, f32[1]{0:T(128)} %bitcast.378, f32[1]{0:T(128)} %bitcast.379, f32[1]{0:T(128)} %bitcast.380, f32[1]{0:T(128)} %bitcast.381, f32[1]{0:T(128)} %bitcast.382, ...), dimensions={0} | concatenate | bytes 216 | tf_op jit(solution)/shard_map/stack | solution.py:49
  930.0 16.9 %fusion.363 = f32[8,16,128]{2,1,0:T(8,128)S(1)} fusion(f32[10,18,130]{2,1,0:T(8,128)S(1)} %select_maximum_fusion.8, f32[10,17,128]{2,1,0:T(8,128)S(1)} %get-tuple-element.375, f32[1,16,128]{2,1,0:T(8,128)S(1)} %collective-permute-done.89, f32[8,16,128]{2,1,0:T(8,128)S(1)} %get-tuple-element.336, f32[10,17,128]{2,1,0:T(8,128)S(1)} %get-tuple-element.374, ...), kind=kLoop, calls=%fused_computation.867 | loop fusion | flops 950272 | bytes 1851500 | tf_op jit(solution)/shard_map/mul | solution.py:252
  948.3 4.5 collective-permute-start.93
  953.7 17.1 %stack.1037 = f32[27]{0:T(128)S(1)} concatenate(f32[1]{0:T(128)} %bitcast.344, f32[1]{0:T(128)} %bitcast.345, f32[1]{0:T(128)} %bitcast.346, f32[1]{0:T(128)} %bitcast.347, f32[1]{0:T(128)} %bitcast.348, f32[1]{0:T(128)} %bitcast.349, f32[1]{0:T(128)} %bitcast.350, f32[1]{0:T(128)} %bitcast.351, f32[1]{0:T(128)} %bitcast.352, f32[1]{0:T(128)} %bitcast.353, f32[1]{0:T(128)} %bitcast.354, ...), dimensions={0} | concatenate | bytes 216 | tf_op jit(solution)/shard_map/stack | solution.py:49
  970.9 5.1 collective-permute-start.95
  978.5 17.1 %stack.1008 = f32[27]{0:T(128)S(1)} concatenate(f32[1]{0:T(128)} %bitcast.316, f32[1]{0:T(128)} %bitcast.317, f32[1]{0:T(128)} %bitcast.318, f32[1]{0:T(128)} %bitcast.319, f32[1]{0:T(128)} %bitcast.320, f32[1]{0:T(128)} %bitcast.321, f32[1]{0:T(128)} %bitcast.322, f32[1]{0:T(128)} %bitcast.323, f32[1]{0:T(128)} %bitcast.324, f32[1]{0:T(128)} %bitcast.325, f32[1]{0:T(128)} %bitcast.326, ...), dimensions={0} | concatenate | bytes 216 | tf_op jit(solution)/shard_map/stack | solution.py:49
  1005.5 17.0 %stack.979 = f32[27]{0:T(128)S(1)} concatenate(f32[1]{0:T(128)} %bitcast.288, f32[1]{0:T(128)} %bitcast.289, f32[1]{0:T(128)} %bitcast.290, f32[1]{0:T(128)} %bitcast.291, f32[1]{0:T(128)} %bitcast.292, f32[1]{0:T(128)} %bitcast.293, f32[1]{0:T(128)} %bitcast.294, f32[1]{0:T(128)} %bitcast.295, f32[1]{0:T(128)} %bitcast.296, f32[1]{0:T(128)} %bitcast.297, f32[1]{0:T(128)} %bitcast.298, ...), dimensions={0} | concatenate | bytes 216 | tf_op jit(solution)/shard_map/stack | solution.py:49
  1022.5 42.6 %psum.7 = f32[9,27]{1,0:T(8,128)S(1)} all-reduce(f32[9,27]{1,0:T(8,128)S(1)} %stack.1268), channel_id=1, replica_groups=mesh['gx'=8,'gy'=4] {'gx','gy'}, use_global_device_ids=true, to_apply=%region_307.308 | all-reduce | flops 243 | bytes 1944 | tf_op jit(solution)/shard_map/psum | solution.py:260
  1072.5 18.3 %fusion.175 = f32[16,32,128]{2,1,0:T(8,128)} fusion(f32[18,34,130]{2,1,0:T(8,128)S(1)} %select_maximum_fusion, f32[18,33,128]{2,1,0:T(8,128)S(1)} %get-tuple-element.349, f32[1,32,128]{2,1,0:T(8,128)S(1)} %collective-permute-done.97, f32[16,32,128]{2,1,0:T(8,128)S(1)} %get-tuple-element.337, f32[18,33,128]{2,1,0:T(8,128)S(1)} %get-tuple-element.348, ...), kind=kLoop, calls=%fused_computation.503 | loop fusion | flops 3735552 | bytes 7372908 | tf_op jit(solution)/shard_map/add | solution.py:256
  (622 shorter events, 309.5 us)
Async XLA Ops:
  1.5 32.2 %collective-permute-start.1 = (f32[2,32,128]{2,1,0:T(8,128)S(1)}, f32[2,32,128]{2,1,0:T(8,128)S(1)}, u32[]{:S(2)}, u32[]{:S(2)}) collective-permute-start(f32[2,32,128]{2,1,0:T(8,128)S(1)} %get-tuple-element.360), channel_id=1, source_target_pairs={{4,0},{8,4},{12,8},{16,12},{20,16},{24,20},{28,24},{5,1},{9,5},{13... | collective-permute-start | bytes 98312 | tf_op jit(solution)/shard_map/ppermute | solution.py:18
  2.8 30.3 %collective-permute-start = (f32[2,32,128]{2,1,0:T(8,128)S(1)}, f32[2,32,128]{2,1,0:T(8,128)S(1)}, u32[]{:S(2)}, u32[]{:S(2)}) collective-permute-start(f32[2,32,128]{2,1,0:T(8,128)S(1)} %get-tuple-element.361), channel_id=1, source_target_pairs={{0,4},{4,8},{8,12},{12,16},{16,20},{20,24},{24,28},{1,5},{5,9},{9,... | collective-permute-start | bytes 98312 | tf_op jit(solution)/shard_map/ppermute | solution.py:17
  61.9 6.9 collective-permute-start.4
  66.2 5.6 collective-permute-start.5
  97.2 6.0 collective-permute-start.8
  100.7 5.5 collective-permute-start.9
  131.1 7.5 collective-permute-start.13
  132.4 6.2 collective-permute-start.12
  185.4 5.6 collective-permute-start.17
  208.3 6.8 collective-permute-start.18
  216.1 6.3 collective-permute-start.20
  240.7 5.8 collective-permute-start.22
  247.9 5.9 collective-permute-start.24
  271.7 7.2 collective-permute-start.27
  273.0 5.9 collective-permute-start.26
  278.9 5.8 collective-permute-start.28
  303.3 6.8 collective-permute-start.30
  307.4 5.5 collective-permute-start.31
  313.0 5.7 collective-permute-start.32
  337.6 7.4 collective-permute-start.34
  342.4 5.6 collective-permute-start.35
  348.0 5.6 collective-permute-start.36
  376.2 5.8 collective-permute-start.39
  413.6 5.8 collective-permute-start.43
  449.9 5.6 collective-permute-start.47
  483.2 6.0 collective-permute-start.50
  487.8 5.5 collective-permute-start.51
  520.7 5.8 collective-permute-start.55
  522.0 6.1 collective-permute-start.54
  577.2 5.6 collective-permute-start.59
  600.8 6.2 collective-permute-start.60
  612.1 23.5 %collective-permute-start.62 = (f32[8,1,128]{2,1,0:T(1,128)}, f32[8,1,128]{2,1,0:T(1,128)}, u32[]{:S(2)}, u32[]{:S(2)}) collective-permute-start(f32[8,1,128]{2,1,0:T(1,128)} %get-tuple-element.444), channel_id=1, source_target_pairs={{0,1},{1,2},{2,3},{4,5},{5,6},{6,7},{8,9},{9,10},{10,11},{12,13},{... | collective-permute-start | bytes 12296 | tf_op jit(solution)/shard_map/ppermute | solution.py:17
  615.9 19.7 %collective-permute-start.63 = (f32[8,1,128]{2,1,0:T(1,128)}, f32[8,1,128]{2,1,0:T(1,128)}, u32[]{:S(2)}, u32[]{:S(2)}) collective-permute-start(f32[8,1,128]{2,1,0:T(1,128)} %get-tuple-element.445), channel_id=1, source_target_pairs={{1,0},{2,1},{3,2},{5,4},{6,5},{7,6},{9,8},{10,9},{11,10},{13,12},{... | collective-permute-start | bytes 12296 | tf_op jit(solution)/shard_map/ppermute | solution.py:18
  661.2 6.4 collective-permute-start.66
  686.1 20.0 %collective-permute-start.69 = (f32[1,4,128]{2,1,0:T(4,128)S(1)}, f32[1,4,128]{2,1,0:T(4,128)S(1)}, u32[]{:S(2)}, u32[]{:S(2)}) collective-permute-start(f32[1,4,128]{2,1,0:T(4,128)S(1)} %bitcast.632), channel_id=1, source_target_pairs={{0,4},{4,8},{8,12},{12,16},{16,20},{20,24},{24,28},{1,5},{5,9},{9,... | collective-permute-start | bytes 6152 | tf_op jit(solution)/shard_map/ppermute | solution.py:17
  688.0 18.2 %collective-permute-start.68 = (f32[1,4,128]{2,1,0:T(4,128)S(1)}, f32[1,4,128]{2,1,0:T(4,128)S(1)}, u32[]{:S(2)}, u32[]{:S(2)}) collective-permute-start(f32[1,4,128]{2,1,0:T(4,128)S(1)} %bitcast.633), channel_id=1, source_target_pairs={{4,0},{8,4},{12,8},{16,12},{20,16},{24,20},{28,24},{5,1},{9,5},{13... | collective-permute-start | bytes 6152 | tf_op jit(solution)/shard_map/ppermute | solution.py:18
  706.2 5.8 collective-permute-start.71
  714.5 6.4 collective-permute-start.72
  718.9 5.5 collective-permute-start.73
  724.3 20.9 %collective-permute-start.74 = (f32[4,1,128]{2,1,0:T(1,128)S(1)}, f32[4,1,128]{2,1,0:T(1,128)S(1)}, u32[]{:S(2)}, u32[]{:S(2)}) collective-permute-start(f32[4,1,128]{2,1,0:T(1,128)S(1)} %get-tuple-element.436), channel_id=1, source_target_pairs={{0,1},{1,2},{2,3},{4,5},{5,6},{6,7},{8,9},{9,10},{10,11},{12,13},{... | collective-permute-start | bytes 6152 | tf_op jit(solution)/shard_map/ppermute | solution.py:17
  727.2 18.1 %collective-permute-start.75 = (f32[4,1,128]{2,1,0:T(1,128)S(1)}, f32[4,1,128]{2,1,0:T(1,128)S(1)}, u32[]{:S(2)}, u32[]{:S(2)}) collective-permute-start(f32[4,1,128]{2,1,0:T(1,128)S(1)} %get-tuple-element.437), channel_id=1, source_target_pairs={{1,0},{2,1},{3,2},{5,4},{6,5},{7,6},{9,8},{10,9},{11,10},{13,12},{... | collective-permute-start | bytes 6152 | tf_op jit(solution)/shard_map/ppermute | solution.py:18
  763.1 6.8 collective-permute-start.76
  764.4 5.9 collective-permute-start.77
  770.4 22.3 %collective-permute-start.79 = (f32[6,1,128]{2,1,0:T(1,128)S(1)}, f32[6,1,128]{2,1,0:T(1,128)S(1)}, u32[]{:S(2)}, u32[]{:S(2)}) collective-permute-start(f32[6,1,128]{2,1,0:T(1,128)S(1)} %get-tuple-element.414), channel_id=1, source_target_pairs={{0,1},{1,2},{2,3},{4,5},{5,6},{6,7},{8,9},{9,10},{10,11},{12,13},{... | collective-permute-start | bytes 9224 | tf_op jit(solution)/shard_map/ppermute | solution.py:17
  773.6 19.1 %collective-permute-start.78 = (f32[6,1,128]{2,1,0:T(1,128)S(1)}, f32[6,1,128]{2,1,0:T(1,128)S(1)}, u32[]{:S(2)}, u32[]{:S(2)}) collective-permute-start(f32[6,1,128]{2,1,0:T(1,128)S(1)} %get-tuple-element.415), channel_id=1, source_target_pairs={{1,0},{2,1},{3,2},{5,4},{6,5},{7,6},{9,8},{10,9},{11,10},{13,12},{... | collective-permute-start | bytes 9224 | tf_op jit(solution)/shard_map/ppermute | solution.py:18
  794.2 6.7 collective-permute-start.80
  798.7 6.3 collective-permute-start.81
  805.0 23.6 %collective-permute-start.82 = (f32[6,1,128]{2,1,0:T(1,128)S(1)}, f32[6,1,128]{2,1,0:T(1,128)S(1)}, u32[]{:S(2)}, u32[]{:S(2)}) collective-permute-start(f32[6,1,128]{2,1,0:T(1,128)S(1)} %get-tuple-element.412), channel_id=1, source_target_pairs={{0,1},{1,2},{2,3},{4,5},{5,6},{6,7},{8,9},{9,10},{10,11},{12,13},{... | collective-permute-start | bytes 9224 | tf_op jit(solution)/shard_map/ppermute | solution.py:17
  809.6 19.0 %collective-permute-start.83 = (f32[6,1,128]{2,1,0:T(1,128)S(1)}, f32[6,1,128]{2,1,0:T(1,128)S(1)}, u32[]{:S(2)}, u32[]{:S(2)}) collective-permute-start(f32[6,1,128]{2,1,0:T(1,128)S(1)} %get-tuple-element.413), channel_id=1, source_target_pairs={{1,0},{2,1},{3,2},{5,4},{6,5},{7,6},{9,8},{10,9},{11,10},{13,12},{... | collective-permute-start | bytes 9224 | tf_op jit(solution)/shard_map/ppermute | solution.py:18
  846.3 24.4 %collective-permute-start.84 = (f32[1,16,128]{2,1,0:T(8,128)S(1)}, f32[1,16,128]{2,1,0:T(8,128)S(1)}, u32[]{:S(2)}, u32[]{:S(2)}) collective-permute-start(f32[1,16,128]{2,1,0:T(8,128)S(1)} %bitcast.642), channel_id=1, source_target_pairs={{4,0},{8,4},{12,8},{16,12},{20,16},{24,20},{28,24},{5,1},{9,5},{13... | collective-permute-start | bytes 24584 | tf_op jit(solution)/shard_map/ppermute | solution.py:18
  847.7 23.1 %collective-permute-start.85 = (f32[1,16,128]{2,1,0:T(8,128)S(1)}, f32[1,16,128]{2,1,0:T(8,128)S(1)}, u32[]{:S(2)}, u32[]{:S(2)}) collective-permute-start(f32[1,16,128]{2,1,0:T(8,128)S(1)} %bitcast.643), channel_id=1, source_target_pairs={{0,4},{4,8},{8,12},{12,16},{16,20},{20,24},{24,28},{1,5},{5,9},{9,... | collective-permute-start | bytes 24584 | tf_op jit(solution)/shard_map/ppermute | solution.py:17
  870.8 24.6 %collective-permute-start.87 = (f32[10,1,128]{2,1,0:T(1,128)S(1)}, f32[10,1,128]{2,1,0:T(1,128)S(1)}, u32[]{:S(2)}, u32[]{:S(2)}) collective-permute-start(f32[10,1,128]{2,1,0:T(1,128)S(1)} %get-tuple-element.378), channel_id=1, source_target_pairs={{0,1},{1,2},{2,3},{4,5},{5,6},{6,7},{8,9},{9,10},{10,11},{12,13},{... | collective-permute-start | bytes 15368 | tf_op jit(solution)/shard_map/ppermute | solution.py:17
  876.3 19.2 %collective-permute-start.86 = (f32[10,1,128]{2,1,0:T(1,128)S(1)}, f32[10,1,128]{2,1,0:T(1,128)S(1)}, u32[]{:S(2)}, u32[]{:S(2)}) collective-permute-start(f32[10,1,128]{2,1,0:T(1,128)S(1)} %get-tuple-element.379), channel_id=1, source_target_pairs={{1,0},{2,1},{3,2},{5,4},{6,5},{7,6},{9,8},{10,9},{11,10},{13,12},{... | collective-permute-start | bytes 15368 | tf_op jit(solution)/shard_map/ppermute | solution.py:18
  897.1 5.9 collective-permute-start.88
  901.7 5.5 collective-permute-start.89
  907.2 22.5 %collective-permute-start.90 = (f32[10,1,128]{2,1,0:T(1,128)S(1)}, f32[10,1,128]{2,1,0:T(1,128)S(1)}, u32[]{:S(2)}, u32[]{:S(2)}) collective-permute-start(f32[10,1,128]{2,1,0:T(1,128)S(1)} %get-tuple-element.376), channel_id=1, source_target_pairs={{0,1},{1,2},{2,3},{4,5},{5,6},{6,7},{8,9},{9,10},{10,11},{12,13},{... | collective-permute-start | bytes 15368 | tf_op jit(solution)/shard_map/ppermute | solution.py:17
  910.6 19.1 %collective-permute-start.91 = (f32[10,1,128]{2,1,0:T(1,128)S(1)}, f32[10,1,128]{2,1,0:T(1,128)S(1)}, u32[]{:S(2)}, u32[]{:S(2)}) collective-permute-start(f32[10,1,128]{2,1,0:T(1,128)S(1)} %get-tuple-element.377), channel_id=1, source_target_pairs={{1,0},{2,1},{3,2},{5,4},{6,5},{7,6},{9,8},{10,9},{11,10},{13,12},{... | collective-permute-start | bytes 15368 | tf_op jit(solution)/shard_map/ppermute | solution.py:18
  947.0 23.8 %collective-permute-start.92 = (f32[1,32,128]{2,1,0:T(8,128)S(1)}, f32[1,32,128]{2,1,0:T(8,128)S(1)}, u32[]{:S(2)}, u32[]{:S(2)}) collective-permute-start(f32[1,32,128]{2,1,0:T(8,128)S(1)} %bitcast.638), channel_id=1, source_target_pairs={{4,0},{8,4},{12,8},{16,12},{20,16},{24,20},{28,24},{5,1},{9,5},{13... | collective-permute-start | bytes 49160 | tf_op jit(solution)/shard_map/ppermute | solution.py:18
  948.3 22.5 %collective-permute-start.93 = (f32[1,32,128]{2,1,0:T(8,128)S(1)}, f32[1,32,128]{2,1,0:T(8,128)S(1)}, u32[]{:S(2)}, u32[]{:S(2)}) collective-permute-start(f32[1,32,128]{2,1,0:T(8,128)S(1)} %bitcast.639), channel_id=1, source_target_pairs={{0,4},{4,8},{8,12},{12,16},{16,20},{20,24},{24,28},{1,5},{5,9},{9,... | collective-permute-start | bytes 49160 | tf_op jit(solution)/shard_map/ppermute | solution.py:17
  970.9 24.7 %collective-permute-start.95 = (f32[18,1,128]{2,1,0:T(1,128)S(1)}, f32[18,1,128]{2,1,0:T(1,128)S(1)}, u32[]{:S(2)}, u32[]{:S(2)}) collective-permute-start(f32[18,1,128]{2,1,0:T(1,128)S(1)} %get-tuple-element.352), channel_id=1, source_target_pairs={{0,1},{1,2},{2,3},{4,5},{5,6},{6,7},{8,9},{9,10},{10,11},{12,13},{... | collective-permute-start | bytes 27656 | tf_op jit(solution)/shard_map/ppermute | solution.py:17
  976.1 19.6 %collective-permute-start.94 = (f32[18,1,128]{2,1,0:T(1,128)S(1)}, f32[18,1,128]{2,1,0:T(1,128)S(1)}, u32[]{:S(2)}, u32[]{:S(2)}) collective-permute-start(f32[18,1,128]{2,1,0:T(1,128)S(1)} %get-tuple-element.353), channel_id=1, source_target_pairs={{1,0},{2,1},{3,2},{5,4},{6,5},{7,6},{9,8},{10,9},{11,10},{13,12},{... | collective-permute-start | bytes 27656 | tf_op jit(solution)/shard_map/ppermute | solution.py:18
  998.2 66.9 %collective-permute-start.96 = (f32[1,32,128]{2,1,0:T(8,128)S(1)}, f32[1,32,128]{2,1,0:T(8,128)S(1)}, u32[]{:S(2)}, u32[]{:S(2)}) collective-permute-start(f32[1,32,128]{2,1,0:T(8,128)S(1)} %get-tuple-element.354), channel_id=1, source_target_pairs={{0,4},{4,8},{8,12},{12,16},{16,20},{20,24},{24,28},{1,5},{5,9},{9,... | collective-permute-start | bytes 49160 | tf_op jit(solution)/shard_map/ppermute | solution.py:17
  1001.9 63.2 %collective-permute-start.97 = (f32[1,32,128]{2,1,0:T(8,128)S(1)}, f32[1,32,128]{2,1,0:T(8,128)S(1)}, u32[]{:S(2)}, u32[]{:S(2)}) collective-permute-start(f32[1,32,128]{2,1,0:T(8,128)S(1)} %get-tuple-element.355), channel_id=1, source_target_pairs={{4,0},{8,4},{12,8},{16,12},{20,16},{24,20},{28,24},{5,1},{9,5},{13... | collective-permute-start | bytes 49160 | tf_op jit(solution)/shard_map/ppermute | solution.py:18
  1066.5 5.6 collective-permute-start.99
  (154 other events, 3893.8 us)
where the time goes:
time: 1110 us; the launch traced here: 1090 us
  other arithmetic  455 us (41%)
  starting transfers between devices  248 us (22%)
  local copies, waits for them, and re-layouts  216 us (19%)
  waiting for transfers between devices  86.1 us (8%)
  blocking collectives  81 us (7%)
    another operation x11, local copies, waits for them, and re-layouts, weight_sums(): return jnp.stack(sums)  187 us
    ppermute x50, starting transfers between devices, extended(): before = lax.ppermute(last, axis, up)  182 us
    mul x8, other arithmetic, smooth_then_apply(): smoothed_loop = shifted_sum(deep, weights, wider) * loop_inside(shape)  145 us
    ppermute x50, waiting for transfers between devices, extended(): after = lax.ppermute(initial, axis, down)  83.5 us
    add x5, other arithmetic, shifted_sum(): total + weights[9 * shift_first + 3 * shift_second + shift_third] * window  77.8 us
    ppermute x50, starting transfers between devices, extended(): after = lax.ppermute(initial, axis, down)  65.2 us
    mul x4, other arithmetic, on_device(): grad_remainder = 0.25 * prolong(grad_down)  55.4 us
    add x3, other arithmetic, on_device(): correction = middle + smoothed  51.2 us
  transfers between devices with their start and end apart: 100, of which 38 were waited for; matrix products, arithmetic and copies ran while one was open for 23% of the time, Pallas kernels for 0%

commit v1 on v0

v1 whole, which is shorter than its diff:
```python
import functools

import jax
import jax.numpy as jnp
from jax import lax
from jax.experimental import pallas as pl
from jax.experimental.pallas import tpu as pltpu
from jax.sharding import PartitionSpec as P

LEVELS = 4
SWEEPS = 3
LOCAL = 2
RIM0 = 10
RIM1 = 4
KEEP = 2
ROWS, COLS = 2, 8
PEERS = ("gx", "gy")


def starts(width):
    places = list(range(0, width - 7, 8))
    if width % 8:
        places.append(width - 8)
    return places


def lanes(shape=(8, 128)):
    return lax.broadcasted_iota(jnp.int32, shape, 1)


def sublanes(shape=(8, 128)):
    return lax.broadcasted_iota(jnp.int32, shape, 0)


def from_below(value):
    return jnp.where(lanes(value.shape) == 0, 0.0, pltpu.roll(value, 1, 1))


def from_above(value):
    last = value.shape[1] - 1
    return jnp.where(lanes(value.shape) == last, 0.0, pltpu.roll(value, last, 1))


def weights_of(stencils, row, flip):
    return [stencils[row, 26 - t if flip else t] for t in range(27)]


class Level:
    def __init__(self, walls, first, second, total_first, total_second):
        self.walls = walls
        self.first = first
        self.second = second
        self.total = (total_first, total_second)

    def row_wall(self, row):
        at = self.first + row
        return jnp.where(at == 0, self.walls[0], 0.0) + jnp.where(
            at == self.total[0] - 1, self.walls[1], 0.0
        )

    def row_inside(self, row):
        at = self.first + row
        return (at >= 0) & (at < self.total[0])

    def wall_plane(self, col):
        at = self.second + col + sublanes()
        lane = lanes()
        plane = jnp.where(at == 0, self.walls[2], 0.0)
        plane = plane + jnp.where(at == self.total[1] - 1, self.walls[3], 0.0)
        plane = plane + jnp.where(lane == 0, self.walls[4], 0.0)
        return plane + jnp.where(lane == 127, self.walls[5], 0.0)

    def inside(self, row, col):
        at = self.second + col + sublanes()
        return self.row_inside(row) & (at >= 0) & (at < self.total[1])


def smoothed(source, weights, row, col):
    sums = [None, None, None]
    for a in range(3):
        for b in range(3):
            window = source[row + (a - 1), pl.ds(col + (b - 1), 8), :]
            for c in range(3):
                term = weights[9 * a + 3 * b + c] * window
                sums[c] = term if sums[c] is None else sums[c] + term
    return sums[1] + from_below(sums[0]) + from_above(sums[2])


def applied(source, level, row, col, at_row, at_col):
    here = source[row, pl.ds(col, 8), :]
    beside = source[row - 1, pl.ds(col, 8), :] + source[row + 1, pl.ds(col, 8), :]
    beside = beside + source[row, pl.ds(col - 1, 8), :] + source[row, pl.ds(col + 1, 8), :]
    beside = beside + from_below(here) + from_above(here)
    diagonal = (6.0 - level.row_wall(at_row)) - level.wall_plane(at_col)
    return diagonal * here - beside


def each(rows, cols, zero, body):
    places = starts(cols)

    def step(row, carry):
        for place in places:
            body(row, zero + place)
        return carry

    lax.fori_loop(0, rows, step, 0)


def smooth_into(out, source, weights, level, start, size, origin, zero, masked=True, add=None):
    def body(row, col):
        row, col = row + start[0], col + start[1]
        value = smoothed(source, weights, row, col)
        if masked:
            value = jnp.where(level.inside(row - origin[0], col - origin[1]), value, 0.0)
        if add is not None:
            value = value + add[row, pl.ds(col, 8), :]
        out[row, pl.ds(col, 8), :] = value

    each(size[0], size[1], zero, body)


def remain_into(out, right, source, level, start, size, origin, zero, masked=True):
    def body(row, col):
        row, col = row + start[0], col + start[1]
        value = right[row, pl.ds(col, 8), :] - applied(
            source, level, row, col, row - origin[0], col - origin[1]
        )
        if masked:
            value = jnp.where(level.inside(row - origin[0], col - origin[1]), value, 0.0)
        out[row, pl.ds(col, 8), :] = value

    each(size[0], size[1], zero, body)


def restrict_into(out, place, right, source, line, fine, coarse, start, size, origin, zero, masked):
    wide = starts(2 * size[1])
    narrow = starts(size[1])

    def step(row, carry):
        for col in wide:
            col = col + zero
            total = None
            for half in range(2):
                at_row, at_col = start[0] + 2 * row + half, start[1] + col
                value = right[at_row, pl.ds(at_col, 8), :] - applied(
                    source, fine, at_row, at_col, at_row - origin[0], at_col - origin[1]
                )
                total = value if total is None else total + value
            line[pl.ds(col, 8), :] = total
        for col in narrow:
            value = line[pl.ds(2 * col, 8, stride=2), :] + line[pl.ds(2 * col + 1, 8, stride=2), :]
            value = 0.25 * value
            if masked is not None:
                value = jnp.where(
                    coarse.inside(place[0] + row - masked[0], place[1] + col + zero - masked[1]),
                    value,
                    0.0,
                )
            out[place[0] + row, pl.ds(place[1] + col + zero, 8), :] = value
        return carry

    lax.fori_loop(0, size[0], step, 0)


def prolong_into(out, place, add, source, start, size, line, zero):
    narrow = starts(size[1])
    wide = starts(2 * size[1])

    def step(row, carry):
        for col in narrow:
            value = source[start[0] + row, pl.ds(start[1] + col + zero, 8), :]
            line[pl.ds(2 * col, 8, stride=2), :] = value
            line[pl.ds(2 * col + 1, 8, stride=2), :] = value
        for col in wide:
            value = line[pl.ds(col + zero, 8), :]
            for half in range(2):
                at_row, at_col = place[0] + 2 * row + half, place[1] + col + zero
                out[at_row, pl.ds(at_col, 8), :] = add[at_row, pl.ds(at_col, 8), :] + value
        return carry

    lax.fori_loop(0, size[0], step, 0)


def clear(array):
    rows, cols = array.shape[0], array.shape[1]

    def step(row, carry):
        array[row] = jnp.zeros((cols, 128), jnp.float32)
        return carry

    lax.fori_loop(0, rows, step, 0)


def copy_block(out, out_at, source, source_at, size, zero):
    def body(row, col):
        out[out_at[0] + row, pl.ds(out_at[1] + col, 8), :] = source[
            source_at[0] + row, pl.ds(source_at[1] + col, 8), :
        ]

    each(size[0], size[1], zero, body)


def correlate(first, first_at, second, second_at, size, zero):
    def step(row, sums):
        sums = list(sums)
        for col in range(0, size[1], 8):
            here = first[first_at[0] + row, pl.ds(first_at[1] + col + zero, 8), :]
            moved = (from_above(here), here, from_below(here))
            for a in range(3):
                for b in range(3):
                    window = second[
                        second_at[0] + row + a - 1, pl.ds(second_at[1] + col + zero + (b - 1), 8), :
                    ]
                    for c in range(3):
                        t = 9 * a + 3 * b + c
                        sums[t] = sums[t] + moved[c] * window
        return tuple(sums)

    blank = tuple(jnp.zeros((8, 128), jnp.float32) for _ in range(27))
    return lax.fori_loop(0, size[0], step, blank)


def place_of(shape, mesh_shape, walls):
    gx, gy = lax.axis_index("gx"), lax.axis_index("gy")
    levels = []
    for height in range(LOCAL):
        rows, cols = shape[0] >> height, shape[1] >> height
        levels.append(
            Level(walls, gx * rows, gy * cols, rows * mesh_shape[0], cols * mesh_shape[1])
        )
    return levels


def down_kernel(shape, mesh_shape, flip, *refs):
    (stencils, mask, still, low_first, block, high_first, low_second, high_second) = refs[:8]
    (kept, kept_pre, right1, pre1, right2) = refs[8:13]
    (wide, pre, line) = refs[13:]
    zero = still[0]
    walls = [mask[f].astype(jnp.float32) for f in range(6)]
    fine, middle = place_of(shape, mesh_shape, walls)
    rows, cols = shape[0], shape[1]
    copy_block(wide, (0, RIM0), low_first, (0, 0), (RIM0, cols), zero)
    copy_block(wide, (RIM0, RIM0), block, (0, 0), (rows, cols), zero)
    copy_block(wide, (RIM0 + rows, RIM0), high_first, (0, 0), (RIM0, cols), zero)
    copy_block(wide, (0, 0), low_second, (0, 0), (rows + 2 * RIM0, RIM0), zero)
    copy_block(wide, (0, RIM0 + cols), high_second, (0, 0), (rows + 2 * RIM0, RIM0), zero)
    before = LEVELS if flip else 0
    weights = weights_of(stencils, before, flip)
    origin = (RIM0, RIM0)
    smooth_into(
        pre, wide, weights, fine, (1, 1), (rows + 2 * RIM0 - 2, cols + 2 * RIM0 - 2), origin, zero
    )
    rows1, cols1 = rows // 2, cols // 2
    restrict_into(
        right1, (0, 0), wide, pre, line, fine, middle,
        (RIM0 - 2 * RIM1, RIM0 - 2 * RIM1), (rows1 + 2 * RIM1, cols1 + 2 * RIM1), origin, zero,
        (RIM1, RIM1),
    )
    inner = (RIM0 - KEEP, RIM0 - KEEP)
    size = (rows + 2 * KEEP, cols + 2 * KEEP)
    copy_block(kept, (0, 0), wide, inner, size, zero)
    copy_block(kept_pre, (0, 0), pre, inner, size, zero)
    weights = weights_of(stencils, before + 1, flip)
    clear(pre1)
    origin = (RIM1, RIM1)
    smooth_into(
        pre1, right1, weights, middle, (1, 1), (rows1 + 2 * RIM1 - 2, cols1 + 2 * RIM1 - 2),
        origin, zero,
    )
    restrict_into(
        right2, (0, 0), right1, pre1, line, middle, None, origin, (rows1 // 2, cols1 // 2), origin,
        zero, None,
    )


def up_kernel(shape, mesh_shape, flip, *refs):
    (stencils, mask, still, gathered, kept, kept_pre, right1, pre1) = refs[:8]
    refs = refs[8:]
    if flip:
        (after0_fwd, kept_fwd, after1_fwd, right1_fwd), refs = refs[:4], refs[4:]
        slabs_fwd, refs = refs[:7], refs[7:]
        (answer, sums), refs = refs[:2], refs[2:]
        (after0, after1), refs = refs[:2], refs[2:]
    else:
        (target,), refs = refs[:1], refs[1:]
        (answer, error, after0, after1), refs = refs[:4], refs[4:]
        slabs_fwd = ()
        slabs, refs = refs[:7], refs[7:]
    (right2, mid2, after2, right3, mid3, after3, right4, mid4, rest1, rest2) = refs[:10]
    (mid1, result1, mid0, line) = refs[10:14]
    zero = still[0]
    walls = [mask[f].astype(jnp.float32) for f in range(6)]
    fine, middle = place_of(shape, mesh_shape, walls)
    gx, gy = lax.axis_index("gx"), lax.axis_index("gy")
    across, along = mesh_shape
    rows2, cols2 = shape[0] // 4, shape[1] // 4
    before, later = (LEVELS, 0) if flip else (0, LEVELS)
    origin = (ROWS, COLS)
    for array in (right2, mid2, after2, right3, mid3, after3, right4, mid4, rest1, rest2):
        clear(array)

    def fill(peer, carry):
        for other in range(along):
            for row in range(rows2):
                for col in range(0, cols2, 8):
                    right2[
                        ROWS + peer * rows2 + row, pl.ds(COLS + other * cols2 + col, 8), :
                    ] = gathered[peer * along + other, row, pl.ds(col, 8), :]
        return carry

    lax.fori_loop(0, across, fill, 0)
    grids = []
    for height in range(LOCAL, LEVELS + 1):
        total = ((shape[0] * across) >> height, (shape[1] * along) >> height)
        grids.append(Level(walls, 0, 0, *total))
    arrays = ((right2, mid2, after2), (right3, mid3, after3))
    coarser = (right3, right4)
    for step in range(2):
        right, mid, after = arrays[step]
        level = grids[step]
        weights = weights_of(stencils, before + LOCAL + step, flip)
        smooth_into(mid, right, weights, level, origin, level.total, origin, zero, masked=False)
        half = (level.total[0] // 2, level.total[1] // 2)
        restrict_into(
            coarser[step], origin, right, mid, line, level, None, origin, half, origin, zero, None
        )
    level = grids[2]
    weights = weights_of(stencils, 2 * LEVELS, flip)
    smooth_into(mid4, right4, weights, level, origin, level.total, origin, zero, masked=False)
    for rest in (rest1, rest2):
        remain_into(rest, right4, mid4, level, origin, level.total, origin, zero, masked=False)
        smooth_into(
            mid4, rest, weights, level, origin, level.total, origin, zero, masked=False, add=mid4
        )
    below = mid4
    for step in (1, 0):
        right, mid, after = arrays[step]
        level = grids[step]
        prolong_into(mid, origin, mid, below, origin, grids[step + 1].total, line, zero)
        remain_into(after, right, mid, level, origin, level.total, origin, zero, masked=False)
        weights = weights_of(stencils, later + LOCAL + step, flip)
        smooth_into(
            mid, after, weights, level, origin, level.total, origin, zero, masked=False, add=mid
        )
        below = mid
    rows1, cols1 = shape[0] // 2, shape[1] // 2
    half = RIM1 // 2
    prolong_into(
        mid1, (0, 0), pre1, below,
        (ROWS + gx * rows2 - half, COLS + gy * cols2 - half),
        (rows2 + 2 * half, cols2 + 2 * half), line, zero,
    )
    origin = (RIM1, RIM1)
    remain_into(
        after1, right1, mid1, middle, (2, 2), (rows1 + 2 * RIM1 - 4, cols1 + 2 * RIM1 - 4),
        origin, zero,
    )
    weights = weights_of(stencils, later + 1, flip)
    smooth_into(
        result1, after1, weights, middle, (3, 3), (rows1 + 2 * RIM1 - 6, cols1 + 2 * RIM1 - 6),
        origin, zero, add=mid1,
    )
    rows, cols = shape[0], shape[1]
    prolong_into(mid0, (0, 0), kept_pre, result1, (3, 3), (rows1 + 2, cols1 + 2), line, zero)
    origin = (KEEP, KEEP)
    remain_into(after0, kept, mid0, fine, (1, 1), (rows + 2, cols + 2), origin, zero)
    weights = weights_of(stencils, later, flip)

    def finish(row, col):
        value = smoothed(after0, weights, row + KEEP, col + KEEP)
        value = value + mid0[row + KEEP, pl.ds(col + KEEP, 8), :]
        answer[row, pl.ds(col, 8), :] = value
        if not flip:
            error[row, pl.ds(col, 8), :] = value - target[row, pl.ds(col, 8), :]

    each(rows, cols, zero, finish)
    kept_arrays = (
        (right2, grids[0]), (after2, grids[0]), (right3, grids[1]), (after3, grids[1]),
        (right4, grids[2]), (rest1, grids[2]), (rest2, grids[2]),
    )

    def own(level):
        return level.total[0] // across

    if not flip:
        for slab, (array, level) in zip(slabs, kept_arrays):
            count = own(level)
            for row in range(count + 2):
                slab[row] = array[ROWS - 1 + gx * count + row]
        return
    chosen = jnp.where(gy == 0, 1.0, 0.0)

    def write(row, sums27, scale):
        for t in range(27):
            line[pl.ds(t, 1), :] = jnp.sum(sums27[t], axis=0, keepdims=True)
        ones = jnp.ones((8, 128), jnp.float32)
        total = lax.dot_general(
            ones, line[0:32, :], (((1,), (1,)), ((), ())),
            precision=lax.Precision.HIGHEST, preferred_element_type=jnp.float32,
        )
        sums[row : row + 1, :] = scale * total[0:1, 0:27]

    line[0:32, :] = jnp.zeros((32, 128), jnp.float32)
    mine = (KEEP, KEEP)
    write(LEVELS, correlate(kept, mine, after0_fwd, mine, (rows, cols), zero), 1.0)
    write(0, correlate(after0, mine, kept_fwd, mine, (rows, cols), zero), 1.0)
    mine = (RIM1, RIM1)
    write(LEVELS + 1, correlate(right1, mine, after1_fwd, mine, (rows1, cols1), zero), 4.0)
    write(1, correlate(after1, mine, right1_fwd, mine, (rows1, cols1), zero), 4.0)
    scale = 16.0
    for step in range(2):
        level = grids[step]
        right, mid, after = arrays[step]
        count = own(level)
        start = (ROWS + gx * count, COLS)
        size = (count, level.total[1])
        slab_right, slab_after = slabs_fwd[2 * step], slabs_fwd[2 * step + 1]
        found = correlate(right, start, slab_after, (1, COLS), size, zero)
        write(LEVELS + LOCAL + step, found, chosen * scale)
        found = correlate(after, start, slab_right, (1, COLS), size, zero)
        write(LOCAL + step, found, chosen * scale)
        scale *= 4.0
    level = grids[2]
    count = own(level)
    start = (ROWS + gx * count, COLS)
    size = (count, level.total[1])
    found = None
    for array, slab in ((right4, slabs_fwd[6]), (rest1, slabs_fwd[5]), (rest2, slabs_fwd[4])):
        more = correlate(array, start, slab, (1, COLS), size, zero)
        found = more if found is None else [x + y for x, y in zip(found, more)]
    write(2 * LEVELS, found, chosen * scale)


def spaces(count_smem, arrays):
    smem = [pl.BlockSpec(memory_space=pltpu.SMEM)] * count_smem
    return smem + [pl.BlockSpec(memory_space=pltpu.VMEM)] * (len(arrays) - count_smem)


def call(kernel, outs, scratch, arrays, name):
    return pl.pallas_call(
        kernel,
        out_shape=[jax.ShapeDtypeStruct(shape, jnp.float32) for shape in outs],
        in_specs=spaces(3, arrays),
        out_specs=[pl.BlockSpec(memory_space=pltpu.VMEM)] * len(outs),
        scratch_shapes=[pltpu.VMEM(shape, jnp.float32) for shape in scratch],
        compiler_params=pltpu.CompilerParams(vmem_limit_bytes=60 * 2**20),
        name=name,
    )(*arrays)


def shift_pair(low_part, high_part, axis):
    peers = lax.axis_size(axis)
    up = [(i, i + 1) for i in range(peers - 1)]
    down = [(j, i) for i, j in up]
    return lax.ppermute(high_part, axis, up), lax.ppermute(low_part, axis, down)


def rim(block):
    rows, cols = block.shape[0], block.shape[1]
    low_first, high_first = shift_pair(block[:RIM0], block[rows - RIM0 :], "gx")
    tall_low = jnp.concatenate([low_first[:, :RIM0], block[:, :RIM0], high_first[:, :RIM0]], 0)
    tall_high = jnp.concatenate(
        [low_first[:, cols - RIM0 :], block[:, cols - RIM0 :], high_first[:, cols - RIM0 :]], 0
    )
    low_second, high_second = shift_pair(tall_low, tall_high, "gy")
    return [low_first, block, high_first, low_second, high_second]


def share(block):
    peers = lax.axis_size("gx") * lax.axis_size("gy")
    copies = jnp.broadcast_to(block[None], (peers,) + block.shape)
    return lax.all_to_all(copies, PEERS, 0, 0, tiled=True)


def on_device(rhs, target, stencils, face_mask):
    shape = rhs.shape
    mesh_shape = (lax.axis_size("gx"), lax.axis_size("gy"))
    rows, cols = shape[0], shape[1]
    still = jnp.zeros((1,), jnp.int32)
    small = [stencils, face_mask, still]
    wide = (rows + 2 * RIM0, cols + 2 * RIM0, 128)
    kept = (rows + 2 * KEEP, cols + 2 * KEEP, 128)
    wide1 = (rows // 2 + 2 * RIM1, cols // 2 + 2 * RIM1, 128)
    own2 = (rows // 4, cols // 4, 128)
    totals = [
        ((rows * mesh_shape[0]) >> h, (cols * mesh_shape[1]) >> h) for h in range(LOCAL, LEVELS + 1)
    ]
    whole = [(a + 2 * ROWS, b + 2 * COLS, 128) for a, b in totals]
    slab = [(a // mesh_shape[0] + 2, b + 2 * COLS, 128) for a, b in totals]
    slabs = [slab[0], slab[0], slab[1], slab[1], slab[2], slab[2], slab[2]]
    line = (max(totals[0][1], wide[1], 64), 128)
    scratch = [whole[0]] * 3 + [whole[1]] * 3 + [whole[2]] * 4 + [wide1, wide1, kept, line]

    def down(block, flip):
        return call(
            functools.partial(down_kernel, shape, mesh_shape, flip),
            [kept, kept, wide1, wide1, own2], [wide, wide, line], small + rim(block),
            "down_back" if flip else "down",
        )

    keep0, pre0, right1, pre1, right2 = down(rhs, False)
    answer, error, after0, after1, *kept_slabs = call(
        functools.partial(up_kernel, shape, mesh_shape, False),
        [shape, shape, kept, wide1] + slabs, scratch,
        small + [share(right2), keep0, pre0, right1, pre1, target], "up",
    )
    back0, back_pre0, back1, back_pre1, back2 = down(error, True)
    grad_rhs, sums = call(
        functools.partial(up_kernel, shape, mesh_shape, True),
        [shape, (2 * LEVELS + 1, 27)], [kept, wide1] + scratch,
        small + [share(back2), back0, back_pre0, back1, back_pre1]
        + [after0, keep0, after1, right1] + list(kept_slabs), "up_back",
    )
    cells = rows * mesh_shape[0] * cols * mesh_shape[1] * shape[2]
    grads = jnp.sum(share(sums), axis=0) / cells
    return answer, grad_rhs, grads


def solution(mesh):
    placed = (P("gx", "gy", None), P("gx", "gy", None), P(), P())
    return jax.shard_map(
        on_device,
        mesh=mesh,
        in_specs=placed,
        out_specs=(P("gx", "gy", None), P("gx", "gy", None), P()),
        check_vma=False,
    )
```

time: 1110 us -> 190 us (0.17); the launches traced: 1090 us -> 189 us
  other arithmetic: 455 us -> 1.45 us
  starting transfers between devices: 248 us -> 19.3 us
  local copies, waits for them, and re-layouts: 216 us -> 8.67 us
  Pallas kernels: 0 us -> 83.9 us
  waiting for transfers between devices: 86.1 us -> 13.7 us
  blocking collectives: 81 us -> 61 us
    ppermute x100 -> x8, starting transfers between devices: 248 us -> 19.3 us  [the longest x4 14.1 us: shift_pair(): lax.ppermute(high_part, axis, up)]
    mul x27 -> x0, other arithmetic: 218 us -> none  [the longest x8 145 us: smooth_then_apply(): smoothed_loop = shifted_sum(deep, weights, wider) * loop_inside(shape)]
    another operation x12 -> x0, local copies, waits for them, and re-layouts: 187 us -> none  [the longest x11 187 us: weight_sums(): return jnp.stack(sums)]
    add x23 -> x0, other arithmetic: 175 us -> none  [the longest x5 77.8 us: shifted_sum(): total + weights[9 * shift_first + 3 * shift_second + shift_third] * window]
    pallas_call x0 -> x4, Pallas kernels: none -> 83.9 us  [call(): pl.pallas_call(kernel, out_shape=[jax.ShapeDtypeStruct(shape, jnp.float32...]
    ppermute x100 -> x8, waiting for transfers between devices: 86.1 us -> 13.7 us  [the longest x4 7.67 us: shift_pair(): lax.ppermute(low_part, axis, down)]
    all_to_all x0 -> x3, blocking collectives: none -> 61 us  [share(): return lax.all_to_all(copies, PEERS, 0, 0, tiled=True)]
    reduce_sum x32 -> x1, other arithmetic: 46 us -> 0.04 us  [on_device(): grads = jnp.sum(share(sums), axis=0) / cells]
  transfers between devices with their start and end apart: 100 -> 8, of which waited for: 38 -> 6; matrix products, arithmetic and copies ran while one was open for 23% -> 0% of each run, Pallas kernels for 0% -> 0%
where the time goes in v1:
time: 190 us; the launch traced here: 189 us
  Pallas kernels  83.9 us (44%)
  blocking collectives  61 us (32%)
  starting transfers between devices  19.3 us (10%)
  waiting for transfers between devices  13.7 us (7%)
  local copies, waits for them, and re-layouts  8.67 us (5%)
    pallas_call x4, Pallas kernels, call(): pl.pallas_call(kernel, out_shape=[jax.ShapeDtypeStruct(shape, jnp.float32...  83.9 us
    all_to_all x3, blocking collectives, share(): return lax.all_to_all(copies, PEERS, 0, 0, tiled=True)  61 us
    ppermute x4, starting transfers between devices, shift_pair(): lax.ppermute(high_part, axis, up)  14.1 us
    ppermute x4, waiting for transfers between devices, shift_pair(): lax.ppermute(low_part, axis, down)  7.67 us
    ppermute x4, waiting for transfers between devices, shift_pair(): lax.ppermute(high_part, axis, up)  6.04 us
    ppermute x4, starting transfers between devices, shift_pair(): lax.ppermute(low_part, axis, down)  5.17 us
  transfers between devices with their start and end apart: 8, of which 6 were waited for; matrix products, arithmetic and copies ran while one was open for 0% of the time, Pallas kernels for 0%

profile of v1, /device:TPU:0, one launch (start us, length us, event | category | flops | bytes accessed | tf_op | source)
XLA Modules:
  0.0 188.9 jit_solution(10241234272323052754)
XLA Ops:
  0.6 0.0 copy-start
  0.6 1.1 fusion.3
  1.7 4.9 %collective-permute-start = (f32[10,32,128]{2,1,0:T(8,128)S(1)}, f32[10,32,128]{2,1,0:T(8,128)S(1)}, u32[]{:S(2)}, u32[]{:S(2)}) collective-permute-start(f32[10,32,128]{2,1,0:T(8,128)S(1)} %get-tuple-element.56), channel_id=1, source_target_pairs={{0,4},{4,8},{8,12},{12,16},{16,20},{20,24},{24,28},{1,5},{5,9},{9,... | collective-permute-start | bytes 491528 | tf_op jit(solution)/shard_map/ppermute | solution.py:455
  6.6 1.3 collective-permute-start.1
  7.9 0.0 copy-done
  8.0 2.1 %collective-permute-done.refs_3_ = f32[10,32,128]{2,1,0:T(8,128)S(1)} collective-permute-done((f32[10,32,128]{2,1,0:T(8,128)S(1)}, f32[10,32,128]{2,1,0:T(8,128)S(1)}, u32[]{:S(2)}, u32[]{:S(2)}) %collective-permute-start) | collective-permute-done | bytes 163872 | tf_op jit(solution)/shard_map/ppermute | solution.py:455
  10.0 0.0 copy-start.3
  10.1 4.1 %collective-permute-done.1.refs_5_ = f32[10,32,128]{2,1,0:T(8,128)S(1)} collective-permute-done((f32[10,32,128]{2,1,0:T(8,128)S(1)}, f32[10,32,128]{2,1,0:T(8,128)S(1)}, u32[]{:S(2)}, u32[]{:S(2)}) %collective-permute-start.1) | collective-permute-done | bytes 163872 | tf_op jit(solution)/shard_map/ppermute | solution.py:455
  14.2 0.0 copy-start.5
  14.2 0.0 copy-done.3
  14.2 0.6 copy-done.5
  14.9 1.3 collective-permute-start.3
  16.2 3.0 %collective-permute-start.2 = (f32[36,10,128]{2,1,0:T(8,128)S(1)}, f32[36,10,128]{2,1,0:T(8,128)S(1)}, u32[]{:S(2)}, u32[]{:S(2)}) collective-permute-start(f32[36,10,128]{2,1,0:T(8,128)S(1)} %pad_maximum_fusion), channel_id=1, source_target_pairs={{0,1},{1,2},{2,3},{4,5},{5,6},{6,7},{8,9},{9,10},{10,11},{12,13},{... | collective-permute-start | bytes 552968 | tf_op jit(solution)/shard_map/ppermute | solution.py:455
  19.2 0.0 collective-permute-done.3.refs_7_
  19.3 0.0 copy-start.7
  19.3 1.2 collective-permute-done.2.refs_6_
  20.4 0.0 copy-done.7
  20.4 0.0 copy-start.9
  20.4 0.7 copy-done.9
  21.1 10.5 %down.1 = (f32[20,36,128]{2,1,0:T(8,128)}, f32[20,36,128]{2,1,0:T(8,128)}, f32[16,24,128]{2,1,0:T(8,128)}, f32[16,24,128]{2,1,0:T(8,128)}, f32[4,8,128]{2,1,0:T(8,128)}) custom-call(f32[9,27]{1,0:T(8,128)} %refs_0_.7, s32[6]{0:T(128)} %refs_1_.7, s32[1]{0:T(128)} %constant.1.clone.1.refs_2_, f32[10,32,128]{2,1,0:T(8,128)} %copy-done.3, ...), custom_call_target="tpu_custom_call" | custom-call | tf_op jit(solution)/shard_map/down/pallas_call | solution.py:440
  31.7 0.8 broadcast_in_dim.6
  32.4 26.2 %all_to_all.15.refs_3_ = f32[32,4,8,128]{3,2,1,0:T(8,128)} all-to-all(f32[32,4,8,128]{3,2,1,0:T(8,128)S(1)} %broadcast_in_dim.6), channel_id=1, replica_groups=mesh['gx'=8,'gy'=4] {'gx','gy'}, dimensions={0} | all-to-all | bytes 1048576 | tf_op jit(solution)/shard_map/all_to_all | solution.py:472
  58.7 27.9 %up.1 = (f32[16,32,128]{2,1,0:T(8,128)}, f32[16,32,128]{2,1,0:T(8,128)}, f32[20,36,128]{2,1,0:T(8,128)}, f32[16,24,128]{2,1,0:T(8,128)}, f32[6,48,128]{2,1,0:T(8...) custom-call(f32[9,27]{1,0:T(8,128)} %refs_0_.7, ...), custom_call_target="tpu_custom_call" | custom-call | tf_op jit(solution)/shard_map/up/pallas_call | solution.py:440
  86.6 0.0 copy-start.1
  86.6 1.1 fusion.1
  87.7 3.1 %collective-permute-start.4 = (f32[10,32,128]{2,1,0:T(8,128)S(1)}, f32[10,32,128]{2,1,0:T(8,128)S(1)}, u32[]{:S(2)}, u32[]{:S(2)}) collective-permute-start(f32[10,32,128]{2,1,0:T(8,128)S(1)} %get-tuple-element.52), channel_id=1, source_target_pairs={{0,4},{4,8},{8,12},{12,16},{16,20},{20,24},{24,28},{1,5},{5,9},{9,... | collective-permute-start | bytes 491528 | tf_op jit(solution)/shard_map/ppermute | solution.py:455
  90.9 1.3 collective-permute-start.5
  92.2 0.0 copy-done.1
  92.2 1.6 collective-permute-done.4.refs_3_
  93.8 0.0 copy-start.2
  93.9 0.7 copy-done.2
  94.5 3.6 %collective-permute-done.5.refs_5_ = f32[10,32,128]{2,1,0:T(8,128)S(1)} collective-permute-done((f32[10,32,128]{2,1,0:T(8,128)S(1)}, f32[10,32,128]{2,1,0:T(8,128)S(1)}, u32[]{:S(2)}, u32[]{:S(2)}) %collective-permute-start.5) | collective-permute-done | bytes 163872 | tf_op jit(solution)/shard_map/ppermute | solution.py:455
  98.1 0.0 copy-start.4
  98.1 0.6 copy-done.4
  98.7 1.3 collective-permute-start.7
  100.1 3.0 %collective-permute-start.6 = (f32[36,10,128]{2,1,0:T(8,128)S(1)}, f32[36,10,128]{2,1,0:T(8,128)S(1)}, u32[]{:S(2)}, u32[]{:S(2)}) collective-permute-start(f32[36,10,128]{2,1,0:T(8,128)S(1)} %pad_maximum_fusion.2), channel_id=1, source_target_pairs={{0,1},{1,2},{2,3},{4,5},{5,6},{6,7},{8,9},{9,10},{10,11},{12,13},{... | collective-permute-start | bytes 552968 | tf_op jit(solution)/shard_map/ppermute | solution.py:455
  103.1 0.0 collective-permute-done.7.refs_7_
  103.1 0.0 copy-start.6
  103.2 1.2 collective-permute-done.6.refs_6_
  104.3 0.0 copy-done.6
  104.3 0.0 copy-start.8
  104.3 0.7 copy-done.8
  105.0 10.5 %down_back.1 = (f32[20,36,128]{2,1,0:T(8,128)}, f32[20,36,128]{2,1,0:T(8,128)}, f32[16,24,128]{2,1,0:T(8,128)}, f32[16,24,128]{2,1,0:T(8,128)}, f32[4,8,128]{2,1,0:T(8,128)}) custom-call(f32[9,27]{1,0:T(8,128)} %refs_0_.7, s32[6]{0:T(128)} %refs_1_.7, s32[1]{0:T(128)} %constant.1.clone.1.refs_2_, f32[10,32,128]{2,1,0:T(8,128)} %copy-done.2, ...), custom_call_target="tpu_custom_call" | custom-call | tf_op jit(solution)/shard_map/down_back/pallas_call | solution.py:440
  115.6 0.8 broadcast_in_dim.7
  116.3 24.7 %all_to_all.16.refs_3_ = f32[32,4,8,128]{3,2,1,0:T(8,128)} all-to-all(f32[32,4,8,128]{3,2,1,0:T(8,128)S(1)} %broadcast_in_dim.7), channel_id=1, replica_groups=mesh['gx'=8,'gy'=4] {'gx','gy'}, dimensions={0} | all-to-all | bytes 1048576 | tf_op jit(solution)/shard_map/all_to_all | solution.py:472
  141.1 34.9 %up_back.1 = (f32[16,32,128]{2,1,0:T(8,128)}, f32[9,27]{1,0:T(8,128)}) custom-call(f32[9,27]{1,0:T(8,128)} %refs_0_.7, s32[6]{0:T(128)} %refs_1_.7, s32[1]{0:T(128)} %constant.1.clone.1.refs_2_, f32[32,4,8,128]{3,2,1,0:T(8,128)} %all_to_all.16.refs_3_, f32[20,36,128]{2,1,0:T(8,128)} %get-tuple-element.34.refs_4_, f32[20,36,128]{2,1,0:T(8,128)} %get-tuple-element.35.refs_5_, ...), custom_call_target="tpu_custom_call" | custom-call | tf_op jit(solution)/shard_map/up_back/pallas_call | solution.py:440
  176.0 0.7 broadcast_in_dim.8
  176.7 0.1 reshape.9
  176.8 10.0 %all_to_all.17 = f32[32,1,243]{2,1,0:T(1,128)S(1)} all-to-all(f32[32,1,243]{2,1,0:T(1,128)S(1)} %reshape.9), channel_id=1, replica_groups=mesh['gx'=8,'gy'=4] {'gx','gy'}, dimensions={0} | all-to-all | bytes 62208 | tf_op jit(solution)/shard_map/all_to_all | solution.py:472
  186.9 0.5 broadcast.4
  187.4 0.7 reduce
  188.1 0.1 reshape.10
  188.3 0.6 broadcast_multiply_fusion
  (11 shorter events, 0.2 us)
Async XLA Ops:
  0.6 7.3 %copy-start = (f32[16,32,128]{2,1,0:T(8,128)S(1)}, f32[16,32,128]{2,1,0:T(8,128)}, u32[]{:S(2)}) copy-start(f32[16,32,128]{2,1,0:T(8,128)} %refs_4_.1) | copy-start | bytes 786436
  1.7 8.3 %collective-permute-start = (f32[10,32,128]{2,1,0:T(8,128)S(1)}, f32[10,32,128]{2,1,0:T(8,128)S(1)}, u32[]{:S(2)}, u32[]{:S(2)}) collective-permute-start(f32[10,32,128]{2,1,0:T(8,128)S(1)} %get-tuple-element.56), channel_id=1, source_target_pairs={{0,4},{4,8},{8,12},{12,16},{16,20},{20,24},{24,28},{1,5},{5,9},{9,... | collective-permute-start | bytes 491528 | tf_op jit(solution)/shard_map/ppermute | solution.py:455
  6.6 7.6 %collective-permute-start.1 = (f32[10,32,128]{2,1,0:T(8,128)S(1)}, f32[10,32,128]{2,1,0:T(8,128)S(1)}, u32[]{:S(2)}, u32[]{:S(2)}) collective-permute-start(f32[10,32,128]{2,1,0:T(8,128)S(1)} %get-tuple-element.55), channel_id=1, source_target_pairs={{4,0},{8,4},{12,8},{16,12},{20,16},{24,20},{28,24},{5,1},{9,5},{13... | collective-permute-start | bytes 491528 | tf_op jit(solution)/shard_map/ppermute | solution.py:455
  10.0 4.1 %copy-start.3 = (f32[10,32,128]{2,1,0:T(8,128)}, f32[10,32,128]{2,1,0:T(8,128)S(1)}, u32[]{:S(2)}) copy-start(f32[10,32,128]{2,1,0:T(8,128)S(1)} %collective-permute-done.refs_3_) | copy-start | bytes 491524
  14.2 0.7 copy-start.5
  14.9 4.4 %collective-permute-start.3 = (f32[36,10,128]{2,1,0:T(8,128)S(1)}, f32[36,10,128]{2,1,0:T(8,128)S(1)}, u32[]{:S(2)}, u32[]{:S(2)}) collective-permute-start(f32[36,10,128]{2,1,0:T(8,128)S(1)} %pad_maximum_fusion.1), channel_id=1, source_target_pairs={{1,0},{2,1},{3,2},{5,4},{6,5},{7,6},{9,8},{10,9},{11,10},{13,12},{... | collective-permute-start | bytes 552968 | tf_op jit(solution)/shard_map/ppermute | solution.py:455
  16.2 4.2 %collective-permute-start.2 = (f32[36,10,128]{2,1,0:T(8,128)S(1)}, f32[36,10,128]{2,1,0:T(8,128)S(1)}, u32[]{:S(2)}, u32[]{:S(2)}) collective-permute-start(f32[36,10,128]{2,1,0:T(8,128)S(1)} %pad_maximum_fusion), channel_id=1, source_target_pairs={{0,1},{1,2},{2,3},{4,5},{5,6},{6,7},{8,9},{9,10},{10,11},{12,13},{... | collective-permute-start | bytes 552968 | tf_op jit(solution)/shard_map/ppermute | solution.py:455
  19.3 1.2 copy-start.7
  20.4 0.7 copy-start.9
  86.6 5.5 %copy-start.1 = (f32[16,32,128]{2,1,0:T(8,128)S(1)}, f32[16,32,128]{2,1,0:T(8,128)}, u32[]{:S(2)}) copy-start(f32[16,32,128]{2,1,0:T(8,128)} %get-tuple-element.32.refs_4_) | copy-start | bytes 786436
  87.7 6.1 %collective-permute-start.4 = (f32[10,32,128]{2,1,0:T(8,128)S(1)}, f32[10,32,128]{2,1,0:T(8,128)S(1)}, u32[]{:S(2)}, u32[]{:S(2)}) collective-permute-start(f32[10,32,128]{2,1,0:T(8,128)S(1)} %get-tuple-element.52), channel_id=1, source_target_pairs={{0,4},{4,8},{8,12},{12,16},{16,20},{20,24},{24,28},{1,5},{5,9},{9,... | collective-permute-start | bytes 491528 | tf_op jit(solution)/shard_map/ppermute | solution.py:455
  90.9 7.2 %collective-permute-start.5 = (f32[10,32,128]{2,1,0:T(8,128)S(1)}, f32[10,32,128]{2,1,0:T(8,128)S(1)}, u32[]{:S(2)}, u32[]{:S(2)}) collective-permute-start(f32[10,32,128]{2,1,0:T(8,128)S(1)} %get-tuple-element.51), channel_id=1, source_target_pairs={{4,0},{8,4},{12,8},{16,12},{20,16},{24,20},{28,24},{5,1},{9,5},{13... | collective-permute-start | bytes 491528 | tf_op jit(solution)/shard_map/ppermute | solution.py:455
  93.8 0.7 copy-start.2
  98.1 0.7 copy-start.4
  98.7 4.4 %collective-permute-start.7 = (f32[36,10,128]{2,1,0:T(8,128)S(1)}, f32[36,10,128]{2,1,0:T(8,128)S(1)}, u32[]{:S(2)}, u32[]{:S(2)}) collective-permute-start(f32[36,10,128]{2,1,0:T(8,128)S(1)} %pad_maximum_fusion.3), channel_id=1, source_target_pairs={{1,0},{2,1},{3,2},{5,4},{6,5},{7,6},{9,8},{10,9},{11,10},{13,12},{... | collective-permute-start | bytes 552968 | tf_op jit(solution)/shard_map/ppermute | solution.py:455
  100.1 4.2 %collective-permute-start.6 = (f32[36,10,128]{2,1,0:T(8,128)S(1)}, f32[36,10,128]{2,1,0:T(8,128)S(1)}, u32[]{:S(2)}, u32[]{:S(2)}) collective-permute-start(f32[36,10,128]{2,1,0:T(8,128)S(1)} %pad_maximum_fusion.2), channel_id=1, source_target_pairs={{0,1},{1,2},{2,3},{4,5},{5,6},{6,7},{8,9},{9,10},{10,11},{12,13},{... | collective-permute-start | bytes 552968 | tf_op jit(solution)/shard_map/ppermute | solution.py:455
  103.1 1.2 copy-start.6
  104.3 0.7 copy-start.8

commit v2 on v1

--- a/solution.py
+++ b/solution.py
@@ -15,6 +15,9 @@
 KEEP = 2
 ROWS, COLS = 2, 8
 PEERS = ("gx", "gy")
+SLOTS = 4
+BODY = 48
+NEAR = 2**21
 
 
 def starts(width):
@@ -95,15 +98,29 @@
     return diagonal * here - beside
 
 
+def rows_at_once(rows, chunks):
+    return max(n for n in range(1, rows + 1) if rows % n == 0 and (n == 1 or n * chunks <= BODY))
+
+
+def by_rows(rows, chunks, step):
+    count = rows_at_once(rows, chunks)
+
+    def several(turn, carry):
+        for row in range(count):
+            step(turn * count + row, row % SLOTS)
+        return carry
+
+    lax.fori_loop(0, rows // count, several, 0)
+
+
 def each(rows, cols, zero, body):
     places = starts(cols)
 
-    def step(row, carry):
+    def step(row, slot):
         for place in places:
             body(row, zero + place)
-        return carry
-
-    lax.fori_loop(0, rows, step, 0)
+
+    by_rows(rows, len(places), step)
 
 
 def smooth_into(out, source, weights, level, start, size, origin, zero, masked=True, add=None):
@@ -136,7 +153,7 @@
     wide = starts(2 * size[1])
     narrow = starts(size[1])
 
-    def step(row, carry):
+    def step(row, slot):
         for col in wide:
             col = col + zero
             total = None
@@ -146,9 +163,10 @@
                     source, fine, at_row, at_col, at_row - origin[0], at_col - origin[1]
                 )
                 total = value if total is None else total + value
-            line[pl.ds(col, 8), :] = total
+            line[slot, pl.ds(col, 8), :] = total
         for col in narrow:
-            value = line[pl.ds(2 * col, 8, stride=2), :] + line[pl.ds(2 * col + 1, 8, stride=2), :]
+            value = line[slot, pl.ds(2 * col, 8, stride=2), :]
+            value = value + line[slot, pl.ds(2 * col + 1, 8, stride=2), :]
             value = 0.25 * value
             if masked is not None:
                 value = jnp.where(
@@ -157,38 +175,35 @@
                     0.0,
                 )
             out[place[0] + row, pl.ds(place[1] + col + zero, 8), :] = value
-        return carry
-
-    lax.fori_loop(0, size[0], step, 0)
+
+    by_rows(size[0], 2 * len(wide), step)
 
 
 def prolong_into(out, place, add, source, start, size, line, zero):
     narrow = starts(size[1])
     wide = starts(2 * size[1])
 
-    def step(row, carry):
+    def step(row, slot):
         for col in narrow:
             value = source[start[0] + row, pl.ds(start[1] + col + zero, 8), :]
-            line[pl.ds(2 * col, 8, stride=2), :] = value
-            line[pl.ds(2 * col + 1, 8, stride=2), :] = value
+            line[slot, pl.ds(2 * col, 8, stride=2), :] = value
+            line[slot, pl.ds(2 * col + 1, 8, stride=2), :] = value
         for col in wide:
-            value = line[pl.ds(col + zero, 8), :]
+            value = line[slot, pl.ds(col + zero, 8), :]
             for half in range(2):
                 at_row, at_col = place[0] + 2 * row + half, place[1] + col + zero
                 out[at_row, pl.ds(at_col, 8), :] = add[at_row, pl.ds(at_col, 8), :] + value
-        return carry
-
-    lax.fori_loop(0, size[0], step, 0)
+
+    by_rows(size[0], len(wide), step)
 
 
 def clear(array):
     rows, cols = array.shape[0], array.shape[1]
 
-    def step(row, carry):
+    def step(row, slot):
         array[row] = jnp.zeros((cols, 128), jnp.float32)
-        return carry
-
-    lax.fori_loop(0, rows, step, 0)
+
+    by_rows(rows, cols // 8, step)
 
 
 def copy_block(out, out_at, source, source_at, size, zero):
@@ -201,9 +216,12 @@
 
 
 def correlate(first, first_at, second, second_at, size, zero):
-    def step(row, sums):
+    cols = range(0, size[1], 8)
+    count = rows_at_once(size[0], len(cols))
+
+    def step(turn, sums):
         sums = list(sums)
-        for col in range(0, size[1], 8):
+        for row, col in [(turn * count + more, col) for more in range(count) for col in cols]:
             here = first[first_at[0] + row, pl.ds(first_at[1] + col + zero, 8), :]
             moved = (from_above(here), here, from_below(here))
             for a in range(3):
@@ -217,7 +235,7 @@
         return tuple(sums)
 
     blank = tuple(jnp.zeros((8, 128), jnp.float32) for _ in range(27))
-    return lax.fori_loop(0, size[0], step, blank)
+    return lax.fori_loop(0, size[0] // count, step, blank)
 
 
 def place_of(shape, mesh_shape, walls):
@@ -390,17 +408,14 @@
         return
     chosen = jnp.where(gy == 0, 1.0, 0.0)
 
-    def write(row, sums27, scale):
+    (part,) = refs[14:]
+
+    def write(row, found, scale):
         for t in range(27):
-            line[pl.ds(t, 1), :] = jnp.sum(sums27[t], axis=0, keepdims=True)
-        ones = jnp.ones((8, 128), jnp.float32)
-        total = lax.dot_general(
-            ones, line[0:32, :], (((1,), (1,)), ((), ())),
-            precision=lax.Precision.HIGHEST, preferred_element_type=jnp.float32,
-        )
-        sums[row : row + 1, :] = scale * total[0:1, 0:27]
-
-    line[0:32, :] = jnp.zeros((32, 128), jnp.float32)
+            part[pl.ds(8 * (32 * row + t), 8), :] = scale * found[t]
+        for t in range(27, 32):
+            part[pl.ds(8 * (32 * row + t), 8), :] = jnp.zeros((8, 128), jnp.float32)
+
     mine = (KEEP, KEEP)
     write(LEVELS, correlate(kept, mine, after0_fwd, mine, (rows, cols), zero), 1.0)
     write(0, correlate(after0, mine, kept_fwd, mine, (rows, cols), zero), 1.0)
@@ -429,6 +444,17 @@
         more = correlate(array, start, slab, (1, COLS), size, zero)
         found = more if found is None else [x + y for x, y in zip(found, more)]
     write(2 * LEVELS, found, chosen * scale)
+    ones = jnp.ones((8, 128), jnp.float32)
+    for row in range(2 * LEVELS + 1):
+        folded = None
+        for fold in range(8):
+            more = part[pl.ds(8 * 32 * row + fold, 32, stride=8), :]
+            folded = more if folded is None else folded + more
+        total = lax.dot_general(
+            ones, folded, (((1,), (1,)), ((), ())),
+            precision=lax.Precision.HIGHEST, preferred_element_type=jnp.float32,
+        )
+        sums[row : row + 1, :] = total[0:1, 0:27]
 
 
 def spaces(count_smem, arrays):
@@ -436,14 +462,37 @@
     return smem + [pl.BlockSpec(memory_space=pltpu.VMEM)] * (len(arrays) - count_smem)
 
 
-def call(kernel, outs, scratch, arrays, name):
+def padded(shape):
+    whole = 4 * -(-shape[-1] // 128) * 128 * -(-shape[-2] // 8) * 8
+    for size in shape[:-2]:
+        whole *= size
+    return whole
+
+
+def near_enough(arrays):
+    return max(padded(x.shape) for x in arrays[3:]) <= NEAR
+
+
+def call(kernel, outs, scratch, arrays, name, far=()):
+    arrays = list(arrays)
+    near = near_enough(arrays)
+    if near:
+        arrays[3:] = [pltpu.with_memory_space_constraint(x, pltpu.VMEM) for x in arrays[3:]]
+    made = [
+        pltpu.VMEM(shape, jnp.float32)
+        if near and place not in far
+        else jax.ShapeDtypeStruct(shape, jnp.float32)
+        for place, shape in enumerate(outs)
+    ]
+    held = sum(padded(shape) for shape in list(outs) + list(scratch))
+    held += sum(padded(x.shape) for x in arrays[3:])
     return pl.pallas_call(
         kernel,
-        out_shape=[jax.ShapeDtypeStruct(shape, jnp.float32) for shape in outs],
+        out_shape=made,
         in_specs=spaces(3, arrays),
         out_specs=[pl.BlockSpec(memory_space=pltpu.VMEM)] * len(outs),
         scratch_shapes=[pltpu.VMEM(shape, jnp.float32) for shape in scratch],
-        compiler_params=pltpu.CompilerParams(vmem_limit_bytes=60 * 2**20),
+        compiler_params=pltpu.CompilerParams(vmem_limit_bytes=min(60 * 2**20, held + 4 * 2**20)),
         name=name,
     )(*arrays)
 
@@ -488,7 +537,8 @@
     whole = [(a + 2 * ROWS, b + 2 * COLS, 128) for a, b in totals]
     slab = [(a // mesh_shape[0] + 2, b + 2 * COLS, 128) for a, b in totals]
     slabs = [slab[0], slab[0], slab[1], slab[1], slab[2], slab[2], slab[2]]
-    line = (max(totals[0][1], wide[1], 64), 128)
+    line = (SLOTS, -(-max(totals[0][1], wide[1]) // 8) * 8, 128)
+    part = ((2 * LEVELS + 1) * 32 * 8, 128)
     scratch = [whole[0]] * 3 + [whole[1]] * 3 + [whole[2]] * 4 + [wide1, wide1, kept, line]
 
     def down(block, flip):
@@ -502,14 +552,14 @@
     answer, error, after0, after1, *kept_slabs = call(
         functools.partial(up_kernel, shape, mesh_shape, False),
         [shape, shape, kept, wide1] + slabs, scratch,
-        small + [share(right2), keep0, pre0, right1, pre1, target], "up",
+        small + [share(right2), keep0, pre0, right1, pre1, target], "up", (0,),
     )
     back0, back_pre0, back1, back_pre1, back2 = down(error, True)
     grad_rhs, sums = call(
         functools.partial(up_kernel, shape, mesh_shape, True),
-        [shape, (2 * LEVELS + 1, 27)], [kept, wide1] + scratch,
+        [shape, (2 * LEVELS + 1, 27)], [kept, wide1] + scratch + [part],
         small + [share(back2), back0, back_pre0, back1, back_pre1]
-        + [after0, keep0, after1, right1] + list(kept_slabs), "up_back",
+        + [after0, keep0, after1, right1] + list(kept_slabs), "up_back", (0,),
     )
     cells = rows * mesh_shape[0] * cols * mesh_shape[1] * shape[2]
     grads = jnp.sum(share(sums), axis=0) / cells

time: 190 us -> 125 us (0.66)
  Pallas kernels: 83.9 us -> 26 us
  local copies, waits for them, and re-layouts: 8.67 us -> 2.12 us
    pallas_call x4, Pallas kernels: 83.9 us -> 26 us  [call(): pl.pallas_call(kernel, out_shape=made, in_specs=spaces(3, arrays), out_sp...]
    unnamed x22 -> x10, local copies, waits for them, and re-layouts: 3.66 us -> 0.29 us
    broadcast_in_dim x3, local copies, waits for them, and re-layouts: 2.24 us -> 0.12 us  [share(): copies = jnp.broadcast_to(block[None], (peers,) + block.shape)]
where the time goes in v2:
time: 125 us
  blocking collectives  60.8 us (49%)
  Pallas kernels  26 us (21%)
  starting transfers between devices  19.3 us (15%)
  waiting for transfers between devices  14.4 us (12%)
  local copies, waits for them, and re-layouts  2.12 us (2%)
  other arithmetic  1.45 us (1%)
    all_to_all x3, blocking collectives, share(): return lax.all_to_all(copies, PEERS, 0, 0, tiled=True)  60.8 us
    pallas_call x4, Pallas kernels, call(): pl.pallas_call(kernel, out_shape=made, in_specs=spaces(3, arrays), out_sp...  26 us
    ppermute x4, starting transfers between devices, shift_pair(): lax.ppermute(high_part, axis, up)  14.1 us
    ppermute x4, waiting for transfers between devices, shift_pair(): lax.ppermute(low_part, axis, down)  8.32 us
    ppermute x4, waiting for transfers between devices, shift_pair(): lax.ppermute(high_part, axis, up)  6.07 us
    ppermute x4, starting transfers between devices, shift_pair(): lax.ppermute(low_part, axis, down)  5.17 us
  transfers between devices with their start and end apart: 8, of which 6 were waited for; matrix products, arithmetic and copies ran while one was open for 0% of the time, Pallas kernels for 0%

profile of v2, /device:TPU:0, one launch (start us, length us, event | category | flops | bytes accessed | tf_op | source)
XLA Modules:
  0.0 125.0 jit_solution(6647963658624857501)
XLA Ops:
  0.6 0.0 copy-start
  0.6 1.1 fusion.3
  1.7 4.9 %collective-permute-start = (f32[10,32,128]{2,1,0:T(8,128)S(1)}, f32[10,32,128]{2,1,0:T(8,128)S(1)}, u32[]{:S(2)}, u32[]{:S(2)}) collective-permute-start(f32[10,32,128]{2,1,0:T(8,128)S(1)} %get-tuple-element.56), channel_id=1, source_target_pairs={{0,4},{4,8},{8,12},{12,16},{16,20},{20,24},{24,28},{1,5},{5,9},{9,... | collective-permute-start | bytes 491528 | tf_op jit(solution)/shard_map/ppermute | solution.py:504
  6.6 1.3 %collective-permute-start.1 = (f32[10,32,128]{2,1,0:T(8,128)S(1)}, f32[10,32,128]{2,1,0:T(8,128)S(1)}, u32[]{:S(2)}, u32[]{:S(2)}) collective-permute-start(f32[10,32,128]{2,1,0:T(8,128)S(1)} %get-tuple-element.55), channel_id=1, source_target_pairs={{4,0},{8,4},{12,8},{16,12},{20,16},{24,20},{28,24},{5,1},{9,5},{13... | collective-permute-start | bytes 491528 | tf_op jit(solution)/shard_map/ppermute | solution.py:504
  7.9 0.0 copy-done
  7.9 2.1 %collective-permute-done.refs_3_ = f32[10,32,128]{2,1,0:T(8,128)S(1)} collective-permute-done((f32[10,32,128]{2,1,0:T(8,128)S(1)}, f32[10,32,128]{2,1,0:T(8,128)S(1)}, u32[]{:S(2)}, u32[]{:S(2)}) %collective-permute-start) | collective-permute-done | bytes 163872 | tf_op jit(solution)/shard_map/ppermute | solution.py:504
  10.1 4.1 %collective-permute-done.1.refs_5_ = f32[10,32,128]{2,1,0:T(8,128)S(1)} collective-permute-done((f32[10,32,128]{2,1,0:T(8,128)S(1)}, f32[10,32,128]{2,1,0:T(8,128)S(1)}, u32[]{:S(2)}, u32[]{:S(2)}) %collective-permute-start.1) | collective-permute-done | bytes 163872 | tf_op jit(solution)/shard_map/ppermute | solution.py:504
  14.2 1.3 %collective-permute-start.3 = (f32[36,10,128]{2,1,0:T(8,128)S(1)}, f32[36,10,128]{2,1,0:T(8,128)S(1)}, u32[]{:S(2)}, u32[]{:S(2)}) collective-permute-start(f32[36,10,128]{2,1,0:T(8,128)S(1)} %pad_maximum_fusion.1), channel_id=1, source_target_pairs={{1,0},{2,1},{3,2},{5,4},{6,5},{7,6},{9,8},{10,9},{11,10},{13,12},{... | collective-permute-start | bytes 552968 | tf_op jit(solution)/shard_map/ppermute | solution.py:504
  15.5 0.0 copy-start.2
  15.5 0.0 copy-start.3
  15.6 3.0 %collective-permute-start.2 = (f32[36,10,128]{2,1,0:T(8,128)S(1)}, f32[36,10,128]{2,1,0:T(8,128)S(1)}, u32[]{:S(2)}, u32[]{:S(2)}) collective-permute-start(f32[36,10,128]{2,1,0:T(8,128)S(1)} %pad_maximum_fusion), channel_id=1, source_target_pairs={{0,1},{1,2},{2,3},{4,5},{5,6},{6,7},{8,9},{9,10},{10,11},{12,13},{... | collective-permute-start | bytes 552968 | tf_op jit(solution)/shard_map/ppermute | solution.py:504
  18.6 0.0 collective-permute-done.3.refs_7_
  18.6 1.2 collective-permute-done.2.refs_6_
  19.8 0.0 copy-done.2
  19.8 0.0 copy-done.3
  19.8 4.5 %down.1 = (f32[20,36,128]{2,1,0:T(8,128)S(1)}, f32[20,36,128]{2,1,0:T(8,128)S(1)}, f32[16,24,128]{2,1,0:T(8,128)S(1)}, f32[16,24,128]{2,1,0:T(8,128)S(1)}, f32[4,8,128]{2,1,0:T(8,128)S(1)}) custom-call(f32[9,27]{1,0:T(8,128)S(1)} %copy-done.2, s32[6]{0:T(128)S(1)} %copy-done.3, s32[1]{0:T(128)} %constant.1.clone.1.refs_2_, ...), custom_call_target="tpu_custom_call" | custom-call | tf_op jit(solution)/shard_map/down/pallas_call | solution.py:489
  24.3 0.1 broadcast_in_dim.6
  24.3 0.0 copy-start.1
  24.4 26.1 %all_to_all.15.refs_3_ = f32[32,4,8,128]{3,2,1,0:T(8,128)S(1)} all-to-all(f32[32,4,8,128]{3,2,1,0:T(8,128)S(1)} %broadcast_in_dim.6), channel_id=1, replica_groups=mesh['gx'=8,'gy'=4] {'gx','gy'}, dimensions={0} | all-to-all | bytes 1048576 | tf_op jit(solution)/shard_map/all_to_all | solution.py:521
  50.5 0.0 copy-done.1
  50.5 7.6 %up.1 = (f32[16,32,128]{2,1,0:T(8,128)}, f32[16,32,128]{2,1,0:T(8,128)S(1)}, f32[20,36,128]{2,1,0:T(8,128)S(1)}, f32[16,24,128]{2,1,0:T(8,128)S(1)}, f32[6,48,12...) custom-call(f32[9,27]{1,0:T(8,128)S(1)} %copy-done.2, ...), custom_call_target="tpu_custom_call" | custom-call | tf_op jit(solution)/shard_map/up/pallas_call | solution.py:489
  58.1 3.1 %collective-permute-start.4 = (f32[10,32,128]{2,1,0:T(8,128)S(1)}, f32[10,32,128]{2,1,0:T(8,128)S(1)}, u32[]{:S(2)}, u32[]{:S(2)}) collective-permute-start(f32[10,32,128]{2,1,0:T(8,128)S(1)} %get-tuple-element.52), channel_id=1, source_target_pairs={{0,4},{4,8},{8,12},{12,16},{16,20},{20,24},{24,28},{1,5},{5,9},{9,... | collective-permute-start | bytes 491528 | tf_op jit(solution)/shard_map/ppermute | solution.py:504
  61.2 1.3 %collective-permute-start.5 = (f32[10,32,128]{2,1,0:T(8,128)S(1)}, f32[10,32,128]{2,1,0:T(8,128)S(1)}, u32[]{:S(2)}, u32[]{:S(2)}) collective-permute-start(f32[10,32,128]{2,1,0:T(8,128)S(1)} %get-tuple-element.51), channel_id=1, source_target_pairs={{4,0},{8,4},{12,8},{16,12},{20,16},{24,20},{28,24},{5,1},{9,5},{13... | collective-permute-start | bytes 491528 | tf_op jit(solution)/shard_map/ppermute | solution.py:504
  62.6 1.7 %collective-permute-done.4.refs_3_ = f32[10,32,128]{2,1,0:T(8,128)S(1)} collective-permute-done((f32[10,32,128]{2,1,0:T(8,128)S(1)}, f32[10,32,128]{2,1,0:T(8,128)S(1)}, u32[]{:S(2)}, u32[]{:S(2)}) %collective-permute-start.4) | collective-permute-done | bytes 163872 | tf_op jit(solution)/shard_map/ppermute | solution.py:504
  64.2 4.2 %collective-permute-done.5.refs_5_ = f32[10,32,128]{2,1,0:T(8,128)S(1)} collective-permute-done((f32[10,32,128]{2,1,0:T(8,128)S(1)}, f32[10,32,128]{2,1,0:T(8,128)S(1)}, u32[]{:S(2)}, u32[]{:S(2)}) %collective-permute-start.5) | collective-permute-done | bytes 163872 | tf_op jit(solution)/shard_map/ppermute | solution.py:504
  68.5 1.3 %collective-permute-start.7 = (f32[36,10,128]{2,1,0:T(8,128)S(1)}, f32[36,10,128]{2,1,0:T(8,128)S(1)}, u32[]{:S(2)}, u32[]{:S(2)}) collective-permute-start(f32[36,10,128]{2,1,0:T(8,128)S(1)} %pad_maximum_fusion.3), channel_id=1, source_target_pairs={{1,0},{2,1},{3,2},{5,4},{6,5},{7,6},{9,8},{10,9},{11,10},{13,12},{... | collective-permute-start | bytes 552968 | tf_op jit(solution)/shard_map/ppermute | solution.py:504
  69.8 3.0 %collective-permute-start.6 = (f32[36,10,128]{2,1,0:T(8,128)S(1)}, f32[36,10,128]{2,1,0:T(8,128)S(1)}, u32[]{:S(2)}, u32[]{:S(2)}) collective-permute-start(f32[36,10,128]{2,1,0:T(8,128)S(1)} %pad_maximum_fusion.2), channel_id=1, source_target_pairs={{0,1},{1,2},{2,3},{4,5},{5,6},{6,7},{8,9},{9,10},{10,11},{12,13},{... | collective-permute-start | bytes 552968 | tf_op jit(solution)/shard_map/ppermute | solution.py:504
  72.9 0.0 collective-permute-done.7.refs_7_
  72.9 1.2 collective-permute-done.6.refs_6_
  74.0 4.5 %down_back.1 = (f32[20,36,128]{2,1,0:T(8,128)S(1)}, f32[20,36,128]{2,1,0:T(8,128)S(1)}, f32[16,24,128]{2,1,0:T(8,128)S(1)}, f32[16,24,128]{2,1,0:T(8,128)S(1)}, f32[4,8,128]{2,1,0:T(8,128)S(1)}) custom-call(f32[9,27]{1,0:T(8,128)S(1)} %copy-done.2, s32[6]{0:T(128)S(1)} %copy-done.3, s32[1]{0:T(128)} %constant.1.clone.1.refs_2_, ...), custom_call_target="tpu_custom_call" | custom-call | tf_op jit(solution)/shard_map/down_back/pallas_call | solution.py:489
  78.5 0.1 broadcast_in_dim.7
  78.6 24.6 %all_to_all.16.refs_3_ = f32[32,4,8,128]{3,2,1,0:T(8,128)S(1)} all-to-all(f32[32,4,8,128]{3,2,1,0:T(8,128)S(1)} %broadcast_in_dim.7), channel_id=1, replica_groups=mesh['gx'=8,'gy'=4] {'gx','gy'}, dimensions={0} | all-to-all | bytes 1048576 | tf_op jit(solution)/shard_map/all_to_all | solution.py:521
  103.2 9.5 %up_back.1 = (f32[16,32,128]{2,1,0:T(8,128)}, f32[9,27]{1,0:T(8,128)S(1)}) custom-call(f32[9,27]{1,0:T(8,128)S(1)} %copy-done.2, s32[6]{0:T(128)S(1)} %copy-done.3, s32[1]{0:T(128)} %constant.1.clone.1.refs_2_, f32[32,4,8,128]{3,2,1,0:T(8,128)S(1)} %all_to_all.16.refs_3_, f32[20,36,128]{2,1,0:T(8,128)S(1)} %get-tuple-element.34.refs_4_, ...), custom_call_target="tpu_custom_call" | custom-call | tf_op jit(solution)/shard_map/up_back/pallas_call | solution.py:489
  112.7 0.1 reshape.9
  112.9 10.0 %all_to_all.17 = f32[32,1,243]{2,1,0:T(1,128)S(1)} all-to-all(f32[32,1,243]{2,1,0:T(1,128)S(1)} %reshape.9), channel_id=1, replica_groups=mesh['gx'=8,'gy'=4] {'gx','gy'}, dimensions={0} | all-to-all | bytes 62208 | tf_op jit(solution)/shard_map/all_to_all | solution.py:521
  122.9 0.5 broadcast.4
  123.4 0.7 reduce
  124.2 0.1 reshape.10
  124.4 0.6 broadcast_multiply_fusion
  (13 shorter events, 0.3 us)
Async XLA Ops:
  0.6 7.3 %copy-start = (f32[16,32,128]{2,1,0:T(8,128)S(1)}, f32[16,32,128]{2,1,0:T(8,128)}, u32[]{:S(2)}) copy-start(f32[16,32,128]{2,1,0:T(8,128)} %refs_4_.1) | copy-start | bytes 786436
  1.7 8.3 %collective-permute-start = (f32[10,32,128]{2,1,0:T(8,128)S(1)}, f32[10,32,128]{2,1,0:T(8,128)S(1)}, u32[]{:S(2)}, u32[]{:S(2)}) collective-permute-start(f32[10,32,128]{2,1,0:T(8,128)S(1)} %get-tuple-element.56), channel_id=1, source_target_pairs={{0,4},{4,8},{8,12},{12,16},{16,20},{20,24},{24,28},{1,5},{5,9},{9,... | collective-permute-start | bytes 491528 | tf_op jit(solution)/shard_map/ppermute | solution.py:504
  6.6 7.6 %collective-permute-start.1 = (f32[10,32,128]{2,1,0:T(8,128)S(1)}, f32[10,32,128]{2,1,0:T(8,128)S(1)}, u32[]{:S(2)}, u32[]{:S(2)}) collective-permute-start(f32[10,32,128]{2,1,0:T(8,128)S(1)} %get-tuple-element.55), channel_id=1, source_target_pairs={{4,0},{8,4},{12,8},{16,12},{20,16},{24,20},{28,24},{5,1},{9,5},{13... | collective-permute-start | bytes 491528 | tf_op jit(solution)/shard_map/ppermute | solution.py:504
  14.2 4.4 %collective-permute-start.3 = (f32[36,10,128]{2,1,0:T(8,128)S(1)}, f32[36,10,128]{2,1,0:T(8,128)S(1)}, u32[]{:S(2)}, u32[]{:S(2)}) collective-permute-start(f32[36,10,128]{2,1,0:T(8,128)S(1)} %pad_maximum_fusion.1), channel_id=1, source_target_pairs={{1,0},{2,1},{3,2},{5,4},{6,5},{7,6},{9,8},{10,9},{11,10},{13,12},{... | collective-permute-start | bytes 552968 | tf_op jit(solution)/shard_map/ppermute | solution.py:504
  15.5 4.3 %copy-start.2 = (f32[9,27]{1,0:T(8,128)S(1)}, f32[9,27]{1,0:T(8,128)}, u32[]{:S(2)}) copy-start(f32[9,27]{1,0:T(8,128)} %refs_0_.7) | copy-start | bytes 2920
  15.5 4.3 %copy-start.3 = (s32[6]{0:T(128)S(1)}, s32[6]{0:T(128)}, u32[]{:S(2)}) copy-start(s32[6]{0:T(128)} %refs_1_.7) | copy-start | bytes 76
  15.6 4.2 %collective-permute-start.2 = (f32[36,10,128]{2,1,0:T(8,128)S(1)}, f32[36,10,128]{2,1,0:T(8,128)S(1)}, u32[]{:S(2)}, u32[]{:S(2)}) collective-permute-start(f32[36,10,128]{2,1,0:T(8,128)S(1)} %pad_maximum_fusion), channel_id=1, source_target_pairs={{0,1},{1,2},{2,3},{4,5},{5,6},{6,7},{8,9},{9,10},{10,11},{12,13},{... | collective-permute-start | bytes 552968 | tf_op jit(solution)/shard_map/ppermute | solution.py:504
  24.3 26.2 %copy-start.1 = (f32[16,32,128]{2,1,0:T(8,128)S(1)}, f32[16,32,128]{2,1,0:T(8,128)}, u32[]{:S(2)}) copy-start(f32[16,32,128]{2,1,0:T(8,128)} %refs_8_.1) | copy-start | bytes 786436
  58.1 6.1 %collective-permute-start.4 = (f32[10,32,128]{2,1,0:T(8,128)S(1)}, f32[10,32,128]{2,1,0:T(8,128)S(1)}, u32[]{:S(2)}, u32[]{:S(2)}) collective-permute-start(f32[10,32,128]{2,1,0:T(8,128)S(1)} %get-tuple-element.52), channel_id=1, source_target_pairs={{0,4},{4,8},{8,12},{12,16},{16,20},{20,24},{24,28},{1,5},{5,9},{9,... | collective-permute-start | bytes 491528 | tf_op jit(solution)/shard_map/ppermute | solution.py:504
  61.2 7.2 %collective-permute-start.5 = (f32[10,32,128]{2,1,0:T(8,128)S(1)}, f32[10,32,128]{2,1,0:T(8,128)S(1)}, u32[]{:S(2)}, u32[]{:S(2)}) collective-permute-start(f32[10,32,128]{2,1,0:T(8,128)S(1)} %get-tuple-element.51), channel_id=1, source_target_pairs={{4,0},{8,4},{12,8},{16,12},{20,16},{24,20},{28,24},{5,1},{9,5},{13... | collective-permute-start | bytes 491528 | tf_op jit(solution)/shard_map/ppermute | solution.py:504
  68.5 4.4 %collective-permute-start.7 = (f32[36,10,128]{2,1,0:T(8,128)S(1)}, f32[36,10,128]{2,1,0:T(8,128)S(1)}, u32[]{:S(2)}, u32[]{:S(2)}) collective-permute-start(f32[36,10,128]{2,1,0:T(8,128)S(1)} %pad_maximum_fusion.3), channel_id=1, source_target_pairs={{1,0},{2,1},{3,2},{5,4},{6,5},{7,6},{9,8},{10,9},{11,10},{13,12},{... | collective-permute-start | bytes 552968 | tf_op jit(solution)/shard_map/ppermute | solution.py:504
  69.8 4.2 %collective-permute-start.6 = (f32[36,10,128]{2,1,0:T(8,128)S(1)}, f32[36,10,128]{2,1,0:T(8,128)S(1)}, u32[]{:S(2)}, u32[]{:S(2)}) collective-permute-start(f32[36,10,128]{2,1,0:T(8,128)S(1)} %pad_maximum_fusion.2), channel_id=1, source_target_pairs={{0,1},{1,2},{2,3},{4,5},{5,6},{6,7},{8,9},{9,10},{10,11},{12,13},{... | collective-permute-start | bytes 552968 | tf_op jit(solution)/shard_map/ppermute | solution.py:504

commit v3 on v2

--- a/solution.py
+++ b/solution.py
@@ -14,10 +14,19 @@
 RIM1 = 4
 KEEP = 2
 ROWS, COLS = 2, 8
-PEERS = ("gx", "gy")
+SECOND = ("y", "core")
+PEERS = ("gx",) + SECOND
 SLOTS = 4
-BODY = 48
+BODY = 64
 NEAR = 2**21
+
+
+def second_index():
+    return lax.axis_index("y") * lax.axis_size("core") + lax.axis_index("core")
+
+
+def second_size():
+    return lax.axis_size("y") * lax.axis_size("core")
 
 
 def starts(width):
@@ -239,7 +248,7 @@
 
 
 def place_of(shape, mesh_shape, walls):
-    gx, gy = lax.axis_index("gx"), lax.axis_index("gy")
+    gx, gy = lax.axis_index("gx"), second_index()
     levels = []
     for height in range(LOCAL):
         rows, cols = shape[0] >> height, shape[1] >> height
@@ -292,8 +301,10 @@
 
 
 def up_kernel(shape, mesh_shape, flip, *refs):
-    (stencils, mask, still, gathered, kept, kept_pre, right1, pre1) = refs[:8]
-    refs = refs[8:]
+    (stencils, mask, still), refs = refs[:3], refs[3:]
+    cores = lax.axis_size("core")
+    gathered, refs = refs[:cores], refs[cores:]
+    (kept, kept_pre, right1, pre1), refs = refs[:4], refs[4:]
     if flip:
         (after0_fwd, kept_fwd, after1_fwd, right1_fwd), refs = refs[:4], refs[4:]
         slabs_fwd, refs = refs[:7], refs[7:]
@@ -309,7 +320,7 @@
     zero = still[0]
     walls = [mask[f].astype(jnp.float32) for f in range(6)]
     fine, middle = place_of(shape, mesh_shape, walls)
-    gx, gy = lax.axis_index("gx"), lax.axis_index("gy")
+    gx, gy = lax.axis_index("gx"), second_index()
     across, along = mesh_shape
     rows2, cols2 = shape[0] // 4, shape[1] // 4
     before, later = (LEVELS, 0) if flip else (0, LEVELS)
@@ -318,12 +329,15 @@
         clear(array)
 
     def fill(peer, carry):
-        for other in range(along):
-            for row in range(rows2):
-                for col in range(0, cols2, 8):
-                    right2[
-                        ROWS + peer * rows2 + row, pl.ds(COLS + other * cols2 + col, 8), :
-                    ] = gathered[peer * along + other, row, pl.ds(col, 8), :]
+        for turn, source in enumerate(gathered):
+            core = (lax.axis_index("core") + turn) % cores
+            for other in range(along // cores):
+                start = COLS + (other * cores + core) * cols2
+                for row in range(rows2):
+                    for col in range(0, cols2, 8):
+                        right2[ROWS + peer * rows2 + row, pl.ds(start + col, 8), :] = source[
+                            peer * (along // cores) + other, row, pl.ds(col, 8), :
+                        ]
         return carry
 
     lax.fori_loop(0, across, fill, 0)
@@ -445,16 +459,21 @@
         found = more if found is None else [x + y for x, y in zip(found, more)]
     write(2 * LEVELS, found, chosen * scale)
     ones = jnp.ones((8, 128), jnp.float32)
-    for row in range(2 * LEVELS + 1):
-        folded = None
-        for fold in range(8):
-            more = part[pl.ds(8 * 32 * row + fold, 32, stride=8), :]
-            folded = more if folded is None else folded + more
-        total = lax.dot_general(
-            ones, folded, (((1,), (1,)), ((), ())),
-            precision=lax.Precision.HIGHEST, preferred_element_type=jnp.float32,
-        )
-        sums[row : row + 1, :] = total[0:1, 0:27]
+    folded = None
+    for fold in range(8):
+        more = part[pl.ds(fold, (2 * LEVELS + 1) * 32, stride=8), :]
+        folded = more if folded is None else folded + more
+    total = lax.dot_general(
+        ones, folded, (((1,), (1,)), ((), ())),
+        precision=lax.Precision.HIGHEST, preferred_element_type=jnp.float32,
+    )
+    sums[...] = total[0:1, :]
+
+
+def final_kernel(scale, found, grads):
+    total = jnp.sum(found[...].reshape(found.shape[0], found.shape[2]), axis=0, keepdims=True) * scale
+    for row in range(grads.shape[0]):
+        grads[row : row + 1, :] = total[0:1, 32 * row : 32 * row + grads.shape[1]]
 
 
 def spaces(count_smem, arrays):
@@ -470,14 +489,14 @@
 
 
 def near_enough(arrays):
-    return max(padded(x.shape) for x in arrays[3:]) <= NEAR
-
-
-def call(kernel, outs, scratch, arrays, name, far=()):
+    return max(padded(x.shape) for x in arrays) <= NEAR
+
+
+def call(kernel, outs, scratch, arrays, name, far=(), smem=3):
     arrays = list(arrays)
-    near = near_enough(arrays)
+    near = near_enough(arrays[smem:])
     if near:
-        arrays[3:] = [pltpu.with_memory_space_constraint(x, pltpu.VMEM) for x in arrays[3:]]
+        arrays[smem:] = [pltpu.with_memory_space_constraint(x, pltpu.VMEM) for x in arrays[smem:]]
     made = [
         pltpu.VMEM(shape, jnp.float32)
         if near and place not in far
@@ -485,11 +504,11 @@
         for place, shape in enumerate(outs)
     ]
     held = sum(padded(shape) for shape in list(outs) + list(scratch))
-    held += sum(padded(x.shape) for x in arrays[3:])
+    held += sum(padded(x.shape) for x in arrays[smem:])
     return pl.pallas_call(
         kernel,
         out_shape=made,
-        in_specs=spaces(3, arrays),
+        in_specs=spaces(smem, arrays),
         out_specs=[pl.BlockSpec(memory_space=pltpu.VMEM)] * len(outs),
         scratch_shapes=[pltpu.VMEM(shape, jnp.float32) for shape in scratch],
         compiler_params=pltpu.CompilerParams(vmem_limit_bytes=min(60 * 2**20, held + 4 * 2**20)),
@@ -498,10 +517,13 @@
 
 
 def shift_pair(low_part, high_part, axis):
-    peers = lax.axis_size(axis)
-    up = [(i, i + 1) for i in range(peers - 1)]
-    down = [(j, i) for i, j in up]
-    return lax.ppermute(high_part, axis, up), lax.ppermute(low_part, axis, down)
+    peers = lax.axis_size("gx") if axis == "gx" else second_size()
+    even = (lax.axis_index("gx") if axis == "gx" else second_index()) % 2 == 0
+    found = []
+    for first, sent in ((0, jnp.where(even, high_part, low_part)), (1, jnp.where(even, low_part, high_part))):
+        pairs = [(i, i + 1) for i in range(first, peers - 1, 2)]
+        found.append(lax.ppermute(sent, axis, pairs + [(j, i) for i, j in pairs]))
+    return jnp.where(even, found[1], found[0]), jnp.where(even, found[0], found[1])
 
 
 def rim(block):
@@ -511,19 +533,28 @@
     tall_high = jnp.concatenate(
         [low_first[:, cols - RIM0 :], block[:, cols - RIM0 :], high_first[:, cols - RIM0 :]], 0
     )
-    low_second, high_second = shift_pair(tall_low, tall_high, "gy")
+    low_second, high_second = shift_pair(tall_low, tall_high, SECOND)
     return [low_first, block, high_first, low_second, high_second]
 
 
 def share(block):
-    peers = lax.axis_size("gx") * lax.axis_size("gy")
+    peers = lax.axis_size("gx") * second_size()
     copies = jnp.broadcast_to(block[None], (peers,) + block.shape)
     return lax.all_to_all(copies, PEERS, 0, 0, tiled=True)
 
 
+def share_by_pairs(block):
+    peers = lax.axis_size("gx") * lax.axis_size("y")
+    copies = jnp.broadcast_to(block[None], (peers,) + block.shape)
+    mine = lax.all_to_all(copies, ("gx", "y"), 0, 0, tiled=True)
+    if lax.axis_size("core") == 1:
+        return [mine]
+    return [mine, lax.ppermute(mine, "core", [(0, 1), (1, 0)])]
+
+
 def on_device(rhs, target, stencils, face_mask):
     shape = rhs.shape
-    mesh_shape = (lax.axis_size("gx"), lax.axis_size("gy"))
+    mesh_shape = (lax.axis_size("gx"), second_size())
     rows, cols = shape[0], shape[1]
     still = jnp.zeros((1,), jnp.int32)
     small = [stencils, face_mask, still]
@@ -552,26 +583,32 @@
     answer, error, after0, after1, *kept_slabs = call(
         functools.partial(up_kernel, shape, mesh_shape, False),
         [shape, shape, kept, wide1] + slabs, scratch,
-        small + [share(right2), keep0, pre0, right1, pre1, target], "up", (0,),
+        small + share_by_pairs(right2) + [keep0, pre0, right1, pre1, target], "up", (0,),
     )
     back0, back_pre0, back1, back_pre1, back2 = down(error, True)
     grad_rhs, sums = call(
         functools.partial(up_kernel, shape, mesh_shape, True),
-        [shape, (2 * LEVELS + 1, 27)], [kept, wide1] + scratch + [part],
-        small + [share(back2), back0, back_pre0, back1, back_pre1]
+        [shape, (1, (2 * LEVELS + 1) * 32)], [kept, wide1] + scratch + [part],
+        small + share_by_pairs(back2) + [back0, back_pre0, back1, back_pre1]
         + [after0, keep0, after1, right1] + list(kept_slabs), "up_back", (0,),
     )
     cells = rows * mesh_shape[0] * cols * mesh_shape[1] * shape[2]
-    grads = jnp.sum(share(sums), axis=0) / cells
+    (grads,) = call(
+        functools.partial(final_kernel, 1.0 / cells), [(2 * LEVELS + 1, 27)], [],
+        [share(sums)], "final", (0,), 0,
+    )
     return answer, grad_rhs, grads
 
 
 def solution(mesh):
-    placed = (P("gx", "gy", None), P("gx", "gy", None), P(), P())
+    along = mesh.shape["gy"]
+    cores = 2 if along % 2 == 0 else 1
+    parts = jax.sharding.Mesh(mesh.devices.reshape(-1, along // cores, cores), PEERS)
+    block = P("gx", SECOND, None)
     return jax.shard_map(
         on_device,
-        mesh=mesh,
-        in_specs=placed,
-        out_specs=(P("gx", "gy", None), P("gx", "gy", None), P()),
+        mesh=parts,
+        in_specs=(block, block, P(), P()),
+        out_specs=(block, block, P()),
         check_vma=False,
     )

time: 125 us -> 108 us (0.86)
  starting transfers between devices: 19.3 us -> 6.98 us
  blocking collectives: 60.8 us -> 56.5 us
  local copies, waits for them, and re-layouts: 2.12 us -> 0.83 us
    all_to_all x3 -> x1, blocking collectives: 60.8 us -> 9.67 us  [share(): return lax.all_to_all(copies, PEERS, 0, 0, tiled=True)]
    all_to_all x0 -> x2, blocking collectives: none -> 46.8 us  [share_by_pairs(): mine = lax.all_to_all(copies, ('gx', 'y'), 0, 0, tiled=True)]
    ppermute x8 -> x10, starting transfers between devices: 19.3 us -> 6.98 us  [the longest x8 6.98 us: shift_pair(): found.append(lax.ppermute(sent, axis, pairs + [(j, i) for i, j in pairs]))]
    select_n x0 -> x8, other arithmetic: none -> 1.32 us  [the longest x4 1.19 us: shift_pair(): jnp.where(even, high_part, low_part)]
    ppermute x8 -> x10, waiting for transfers between devices: 14.4 us -> 15.6 us  [the longest x8 12.5 us: shift_pair(): found.append(lax.ppermute(sent, axis, pairs + [(j, i) for i, j in pairs]))]
    pallas_call x4 -> x5, Pallas kernels: 26 us -> 25.9 us  [call(): pl.pallas_call(kernel, out_shape=made, in_specs=spaces(smem, arrays), out...]
  transfers between devices with their start and end apart: 8 -> 10, of which waited for: 6 -> 6; matrix products, arithmetic and copies ran while one was open for 0% -> 0% of each run, Pallas kernels for 0% -> 0%
where the time goes in v3:
time: 108 us
  blocking collectives  56.5 us (52%)
  Pallas kernels  25.9 us (24%)
  waiting for transfers between devices  15.6 us (14%)
  starting transfers between devices  6.98 us (6%)
  other arithmetic  1.34 us (1%)
    all_to_all x2, blocking collectives, share_by_pairs(): mine = lax.all_to_all(copies, ('gx', 'y'), 0, 0, tiled=True)  46.8 us
    pallas_call x5, Pallas kernels, call(): pl.pallas_call(kernel, out_shape=made, in_specs=spaces(smem, arrays), out...  25.9 us
    ppermute x8, waiting for transfers between devices, shift_pair(): found.append(lax.ppermute(sent, axis, pairs + [(j, i) for i, j in pairs]))  12.5 us
    all_to_all x1, blocking collectives, share(): return lax.all_to_all(copies, PEERS, 0, 0, tiled=True)  9.67 us
    ppermute x8, starting transfers between devices, shift_pair(): found.append(lax.ppermute(sent, axis, pairs + [(j, i) for i, j in pairs]))  6.98 us
    ppermute x2, waiting for transfers between devices, share_by_pairs(): return [mine, lax.ppermute(mine, 'core', [(0, 1), (1, 0)])]  3.07 us
  transfers between devices with their start and end apart: 10, of which 6 were waited for; matrix products, arithmetic and copies ran while one was open for 0% of the time, Pallas kernels for 0%

profile of v3, /device:TPU:0, one launch (start us, length us, event | category | flops | bytes accessed | tf_op | source)
XLA Modules:
  0.0 108.0 jit_solution(18062978919156397379)
XLA Ops:
  0.6 0.0 copy-start
  0.7 1.1 slice_select_fusion.2
  1.7 3.0 %collective-permute-start.1 = (f32[10,32,128]{2,1,0:T(8,128)S(1)}, f32[10,32,128]{2,1,0:T(8,128)S(1)}, u32[]{:S(2)}, u32[]{:S(2)}) collective-permute-start(f32[10,32,128]{2,1,0:T(8,128)S(1)} %get-tuple-element.67), channel_id=1, source_target_pairs={{0,4},{8,12},{16,20},{24,28},{4,0},{12,8},{20,16},{28,24},{1,5},{9... | collective-permute-start | bytes 491528 | tf_op jit(solution)/shard_map/ppermute | solution.py:525
  4.8 0.7 collective-permute-start
  5.4 0.0 copy-done
  5.5 6.3 %collective-permute-done.1 = f32[10,32,128]{2,1,0:T(8,128)S(1)} collective-permute-done((f32[10,32,128]{2,1,0:T(8,128)S(1)}, f32[10,32,128]{2,1,0:T(8,128)S(1)}, u32[]{:S(2)}, u32[]{:S(2)}) %collective-permute-start.1) | collective-permute-done | bytes 163872 | tf_op jit(solution)/shard_map/ppermute | solution.py:525
  11.8 0.0 collective-permute-done
  11.9 0.1 collective-permute-start.3
  12.0 0.7 collective-permute-start.2
  12.7 0.9 collective-permute-done.3
  13.5 0.0 collective-permute-done.2
  13.5 0.0 copy-start.2
  13.6 0.0 copy-start.3
  13.6 0.6 copy-done.2
  14.2 0.0 copy-done.3
  14.2 4.5 %down.1 = (f32[20,36,128]{2,1,0:T(8,128)S(1)}, f32[20,36,128]{2,1,0:T(8,128)S(1)}, f32[16,24,128]{2,1,0:T(8,128)S(1)}, f32[16,24,128]{2,1,0:T(8,128)S(1)}, f32[4,8,128]{2,1,0:T(8,128)S(1)}) custom-call(f32[9,27]{1,0:T(8,128)S(1)} %copy-done.2, s32[6]{0:T(128)S(1)} %copy-done.3, s32[1]{0:T(128)} %constant.29.clone.1.refs_2_, ...), custom_call_target="tpu_custom_call" | custom-call | tf_op jit(solution)/shard_map/down/pallas_call | solution.py:508
  18.7 0.0 copy-start.1
  18.7 23.3 %all_to_all.15.refs_3_ = f32[16,4,8,128]{3,2,1,0:T(8,128)S(1)} all-to-all(f32[16,4,8,128]{3,2,1,0:T(8,128)S(1)} %broadcast_in_dim.8), channel_id=1, replica_groups=mesh['gx'=8,'y'=2,'core'=2] {'gx','y'}, dimensions={0} | all-to-all | bytes 524288 | tf_op jit(solution)/shard_map/all_to_all | solution.py:549
  42.1 0.0 collective-permute-start.4
  42.1 1.5 %collective-permute-done.4.refs_4_ = f32[16,4,8,128]{3,2,1,0:T(8,128)S(1)} collective-permute-done((f32[16,4,8,128]{3,2,1,0:T(8,128)S(1)}, f32[16,4,8,128]{3,2,1,0:T(8,128)S(1)}, u32[]{:S(2)}, u32[]{:S(2)}) %collective-permute-start.4) | collective-permute-done | bytes 262176 | tf_op jit(solution)/shard_map/ppermute | solution.py:552
  43.6 0.0 copy-done.1
  43.6 7.2 %up.1 = (f32[16,32,128]{2,1,0:T(8,128)}, f32[16,32,128]{2,1,0:T(8,128)S(1)}, f32[20,36,128]{2,1,0:T(8,128)S(1)}, f32[16,24,128]{2,1,0:T(8,128)S(1)}, f32[6,48,12...) custom-call(f32[9,27]{1,0:T(8,128)S(1)} %copy-done.2, ...), custom_call_target="tpu_custom_call" | custom-call | tf_op jit(solution)/shard_map/up/pallas_call | solution.py:508
  50.8 1.1 %collective-permute-start.6 = (f32[10,32,128]{2,1,0:T(8,128)S(1)}, f32[10,32,128]{2,1,0:T(8,128)S(1)}, u32[]{:S(2)}, u32[]{:S(2)}) collective-permute-start(f32[10,32,128]{2,1,0:T(8,128)S(1)} %get-tuple-element.63), channel_id=1, source_target_pairs={{0,4},{8,12},{16,20},{24,28},{4,0},{12,8},{20,16},{28,24},{1,5},{9... | collective-permute-start | bytes 491528 | tf_op jit(solution)/shard_map/ppermute | solution.py:525
  52.0 0.7 collective-permute-start.5
  52.7 4.5 %collective-permute-done.6 = f32[10,32,128]{2,1,0:T(8,128)S(1)} collective-permute-done((f32[10,32,128]{2,1,0:T(8,128)S(1)}, f32[10,32,128]{2,1,0:T(8,128)S(1)}, u32[]{:S(2)}, u32[]{:S(2)}) %collective-permute-start.6) | collective-permute-done | bytes 163872 | tf_op jit(solution)/shard_map/ppermute | solution.py:525
  57.1 0.0 collective-permute-done.5
  57.3 0.1 collective-permute-start.8
  57.4 0.7 collective-permute-start.7
  58.0 0.9 collective-permute-done.8
  58.9 0.0 collective-permute-done.7
  59.0 4.5 %down_back.1 = (f32[20,36,128]{2,1,0:T(8,128)S(1)}, f32[20,36,128]{2,1,0:T(8,128)S(1)}, f32[16,24,128]{2,1,0:T(8,128)S(1)}, f32[16,24,128]{2,1,0:T(8,128)S(1)}, f32[4,8,128]{2,1,0:T(8,128)S(1)}) custom-call(f32[9,27]{1,0:T(8,128)S(1)} %copy-done.2, s32[6]{0:T(128)S(1)} %copy-done.3, s32[1]{0:T(128)} %constant.29.clone.1.refs_2_, ...), custom_call_target="tpu_custom_call" | custom-call | tf_op jit(solution)/shard_map/down_back/pallas_call | solution.py:508
  63.5 23.5 %all_to_all.16.refs_3_ = f32[16,4,8,128]{3,2,1,0:T(8,128)S(1)} all-to-all(f32[16,4,8,128]{3,2,1,0:T(8,128)S(1)} %broadcast_in_dim.9), channel_id=1, replica_groups=mesh['gx'=8,'y'=2,'core'=2] {'gx','y'}, dimensions={0} | all-to-all | bytes 524288 | tf_op jit(solution)/shard_map/all_to_all | solution.py:549
  87.0 0.0 collective-permute-start.9
  87.0 1.5 %collective-permute-done.9.refs_4_ = f32[16,4,8,128]{3,2,1,0:T(8,128)S(1)} collective-permute-done((f32[16,4,8,128]{3,2,1,0:T(8,128)S(1)}, f32[16,4,8,128]{3,2,1,0:T(8,128)S(1)}, u32[]{:S(2)}, u32[]{:S(2)}) %collective-permute-start.9) | collective-permute-done | bytes 262176 | tf_op jit(solution)/shard_map/ppermute | solution.py:552
  88.5 9.1 %up_back.1 = (f32[16,32,128]{2,1,0:T(8,128)}, f32[1,288]{1,0:T(1,128)S(1)}) custom-call(f32[9,27]{1,0:T(8,128)S(1)} %copy-done.2, s32[6]{0:T(128)S(1)} %copy-done.3, s32[1]{0:T(128)} %constant.29.clone.1.refs_2_, f32[16,4,8,128]{3,2,1,0:T(8,128)S(1)} %all_to_all.16.refs_3_, f32[16,4,8,128]{3,2,1,0:T(8,128)S(1)} %collective-permute-done.9.refs_4_, ...), custom_call_target="tpu_custom_call" | custom-call | tf_op jit(solution)/shard_map/up_back/pallas_call | solution.py:508
  97.6 9.7 %all_to_all.17.found = f32[32,1,288]{2,1,0:T(1,128)S(1)} all-to-all(f32[32,1,288]{2,1,0:T(1,128)S(1)} %broadcast_in_dim.11), channel_id=1, replica_groups=mesh['gx'=8,'y'=2,'core'=2] {'gx','y','core'}, dimensions={0} | all-to-all | bytes 73728 | tf_op jit(solution)/shard_map/all_to_all | solution.py:543
  107.3 0.7 final.1
  (16 shorter events, 0.4 us)
Async XLA Ops:
  0.6 4.8 %copy-start = (f32[16,32,128]{2,1,0:T(8,128)S(1)}, f32[16,32,128]{2,1,0:T(8,128)}, u32[]{:S(2)}) copy-start(f32[16,32,128]{2,1,0:T(8,128)} %refs_4_.1) | copy-start | bytes 786436
  1.7 10.0 %collective-permute-start.1 = (f32[10,32,128]{2,1,0:T(8,128)S(1)}, f32[10,32,128]{2,1,0:T(8,128)S(1)}, u32[]{:S(2)}, u32[]{:S(2)}) collective-permute-start(f32[10,32,128]{2,1,0:T(8,128)S(1)} %get-tuple-element.67), channel_id=1, source_target_pairs={{0,4},{8,12},{16,20},{24,28},{4,0},{12,8},{20,16},{28,24},{1,5},{9... | collective-permute-start | bytes 491528 | tf_op jit(solution)/shard_map/ppermute | solution.py:525
  4.8 7.0 %collective-permute-start = (f32[10,32,128]{2,1,0:T(8,128)S(1)}, f32[10,32,128]{2,1,0:T(8,128)S(1)}, u32[]{:S(2)}, u32[]{:S(2)}) collective-permute-start(f32[10,32,128]{2,1,0:T(8,128)S(1)} %get-tuple-element.68), channel_id=1, source_target_pairs={{4,8},{12,16},{20,24},{8,4},{16,12},{24,20},{5,9},{13,17},{21,25},... | collective-permute-start | bytes 491528 | tf_op jit(solution)/shard_map/ppermute | solution.py:525
  11.9 1.6 %collective-permute-start.3 = (f32[36,10,128]{2,1,0:T(8,128)S(1)}, f32[36,10,128]{2,1,0:T(8,128)S(1)}, u32[]{:S(2)}, u32[]{:S(2)}) collective-permute-start(f32[36,10,128]{2,1,0:T(8,128)S(1)} %get-tuple-element.55), channel_id=1, source_target_pairs={{0,1},{2,3},{1,0},{3,2},{4,5},{6,7},{5,4},{7,6},{8,9},{10,11},{9,8... | collective-permute-start | bytes 552968 | tf_op jit(solution)/shard_map/ppermute | solution.py:525
  12.0 1.6 %collective-permute-start.2 = (f32[36,10,128]{2,1,0:T(8,128)S(1)}, f32[36,10,128]{2,1,0:T(8,128)S(1)}, u32[]{:S(2)}, u32[]{:S(2)}) collective-permute-start(f32[36,10,128]{2,1,0:T(8,128)S(1)} %get-tuple-element.56), channel_id=1, source_target_pairs={{1,2},{2,1},{5,6},{6,5},{9,10},{10,9},{13,14},{14,13},{17,18},{18,... | collective-permute-start | bytes 552968 | tf_op jit(solution)/shard_map/ppermute | solution.py:525
  13.5 0.7 copy-start.2
  13.6 0.7 copy-start.3
  18.7 24.9 %copy-start.1 = (f32[16,32,128]{2,1,0:T(8,128)S(1)}, f32[16,32,128]{2,1,0:T(8,128)}, u32[]{:S(2)}) copy-start(f32[16,32,128]{2,1,0:T(8,128)} %refs_9_.1) | copy-start | bytes 786436
  42.1 1.5 %collective-permute-start.4 = (f32[16,4,8,128]{3,2,1,0:T(8,128)S(1)}, f32[16,4,8,128]{3,2,1,0:T(8,128)S(1)}, u32[]{:S(2)}, u32[]{:S(2)}) collective-permute-start(f32[16,4,8,128]{3,2,1,0:T(8,128)S(1)} %all_to_all.15.refs_3_), channel_id=1, source_target_pairs={{0,1},{1,0},{2,3},{3,2},{4,5},{5,4},{6,7},{7,6},{8,9},{9,8},{10,11... | collective-permute-start | bytes 786440 | tf_op jit(solution)/shard_map/ppermute | solution.py:552
  50.8 6.3 %collective-permute-start.6 = (f32[10,32,128]{2,1,0:T(8,128)S(1)}, f32[10,32,128]{2,1,0:T(8,128)S(1)}, u32[]{:S(2)}, u32[]{:S(2)}) collective-permute-start(f32[10,32,128]{2,1,0:T(8,128)S(1)} %get-tuple-element.63), channel_id=1, source_target_pairs={{0,4},{8,12},{16,20},{24,28},{4,0},{12,8},{20,16},{28,24},{1,5},{9... | collective-permute-start | bytes 491528 | tf_op jit(solution)/shard_map/ppermute | solution.py:525
  52.0 5.2 %collective-permute-start.5 = (f32[10,32,128]{2,1,0:T(8,128)S(1)}, f32[10,32,128]{2,1,0:T(8,128)S(1)}, u32[]{:S(2)}, u32[]{:S(2)}) collective-permute-start(f32[10,32,128]{2,1,0:T(8,128)S(1)} %get-tuple-element.64), channel_id=1, source_target_pairs={{4,8},{12,16},{20,24},{8,4},{16,12},{24,20},{5,9},{13,17},{21,25},... | collective-permute-start | bytes 491528 | tf_op jit(solution)/shard_map/ppermute | solution.py:525
  57.3 1.6 %collective-permute-start.8 = (f32[36,10,128]{2,1,0:T(8,128)S(1)}, f32[36,10,128]{2,1,0:T(8,128)S(1)}, u32[]{:S(2)}, u32[]{:S(2)}) collective-permute-start(f32[36,10,128]{2,1,0:T(8,128)S(1)} %get-tuple-element.51), channel_id=1, source_target_pairs={{0,1},{2,3},{1,0},{3,2},{4,5},{6,7},{5,4},{7,6},{8,9},{10,11},{9,8... | collective-permute-start | bytes 552968 | tf_op jit(solution)/shard_map/ppermute | solution.py:525
  57.4 1.6 %collective-permute-start.7 = (f32[36,10,128]{2,1,0:T(8,128)S(1)}, f32[36,10,128]{2,1,0:T(8,128)S(1)}, u32[]{:S(2)}, u32[]{:S(2)}) collective-permute-start(f32[36,10,128]{2,1,0:T(8,128)S(1)} %get-tuple-element.52), channel_id=1, source_target_pairs={{1,2},{2,1},{5,6},{6,5},{9,10},{10,9},{13,14},{14,13},{17,18},{18,... | collective-permute-start | bytes 552968 | tf_op jit(solution)/shard_map/ppermute | solution.py:525
  87.0 1.5 %collective-permute-start.9 = (f32[16,4,8,128]{3,2,1,0:T(8,128)S(1)}, f32[16,4,8,128]{3,2,1,0:T(8,128)S(1)}, u32[]{:S(2)}, u32[]{:S(2)}) collective-permute-start(f32[16,4,8,128]{3,2,1,0:T(8,128)S(1)} %all_to_all.16.refs_3_), channel_id=1, source_target_pairs={{0,1},{1,0},{2,3},{3,2},{4,5},{5,4},{6,7},{7,6},{8,9},{9,8},{10,11... | collective-permute-start | bytes 786440 | tf_op jit(solution)/shard_map/ppermute | solution.py:552

commit v4 on v3

--- a/solution.py
+++ b/solution.py
@@ -269,8 +269,13 @@
     copy_block(wide, (0, RIM0), low_first, (0, 0), (RIM0, cols), zero)
     copy_block(wide, (RIM0, RIM0), block, (0, 0), (rows, cols), zero)
     copy_block(wide, (RIM0 + rows, RIM0), high_first, (0, 0), (RIM0, cols), zero)
-    copy_block(wide, (0, 0), low_second, (0, 0), (rows + 2 * RIM0, RIM0), zero)
-    copy_block(wide, (0, RIM0 + cols), high_second, (0, 0), (rows + 2 * RIM0, RIM0), zero)
+
+    def side(row, col):
+        at = pl.ds(row * RIM0 + col, 8)
+        wide[row, pl.ds(col, 8), :] = low_second[at, :]
+        wide[row, pl.ds(RIM0 + cols + col, 8), :] = high_second[at, :]
+
+    each(rows + 2 * RIM0, RIM0, zero, side)
     before = LEVELS if flip else 0
     weights = weights_of(stencils, before, flip)
     origin = (RIM0, RIM0)
@@ -533,7 +538,9 @@
     tall_high = jnp.concatenate(
         [low_first[:, cols - RIM0 :], block[:, cols - RIM0 :], high_first[:, cols - RIM0 :]], 0
     )
-    low_second, high_second = shift_pair(tall_low, tall_high, SECOND)
+    low_second, high_second = shift_pair(
+        tall_low.reshape(-1, block.shape[2]), tall_high.reshape(-1, block.shape[2]), SECOND
+    )
     return [low_first, block, high_first, low_second, high_second]
 
 

time: 108 us -> 104 us (0.963)
  blocking collectives: 56.5 us -> 46.4 us
  starting transfers between devices: 6.98 us -> 12 us
    all_to_all x2, blocking collectives: 46.8 us -> 36.7 us  [share_by_pairs(): mine = lax.all_to_all(copies, ('gx', 'y'), 0, 0, tiled=True)]
    ppermute x8, starting transfers between devices: 6.98 us -> 12 us  [shift_pair(): found.append(lax.ppermute(sent, axis, pairs + [(j, i) for i, j in pairs]))]
where the time goes in v4:
time: 104 us; the launch traced here: 103 us
  blocking collectives  46.4 us (45%)
  Pallas kernels  25.6 us (25%)
  waiting for transfers between devices  16.1 us (15%)
  starting transfers between devices  12 us (12%)
  other arithmetic  1.31 us (1%)
    all_to_all x2, blocking collectives, share_by_pairs(): mine = lax.all_to_all(copies, ('gx', 'y'), 0, 0, tiled=True)  36.7 us
    pallas_call x5, Pallas kernels, call(): pl.pallas_call(kernel, out_shape=made, in_specs=spaces(smem, arrays), out...  25.6 us
    ppermute x8, waiting for transfers between devices, shift_pair(): found.append(lax.ppermute(sent, axis, pairs + [(j, i) for i, j in pairs]))  13 us
    ppermute x8, starting transfers between devices, shift_pair(): found.append(lax.ppermute(sent, axis, pairs + [(j, i) for i, j in pairs]))  12 us
    all_to_all x1, blocking collectives, share(): return lax.all_to_all(copies, PEERS, 0, 0, tiled=True)  9.67 us
    ppermute x2, waiting for transfers between devices, share_by_pairs(): return [mine, lax.ppermute(mine, 'core', [(0, 1), (1, 0)])]  3.07 us
  transfers between devices with their start and end apart: 10, of which 6 were waited for; matrix products, arithmetic and copies ran while one was open for 0% of the time, Pallas kernels for 0%

profile of v4, /device:TPU:0, one launch (start us, length us, event | category | flops | bytes accessed | tf_op | source)
XLA Modules:
  0.0 103.2 jit_solution(15787645818627990758)
XLA Ops:
  0.6 0.0 copy-start
  0.7 1.1 %slice_select_fusion.2 = (f32[10,32,128]{2,1,0:T(8,128)S(1)}, f32[10,32,128]{2,1,0:T(8,128)S(1)}) fusion(f32[16,32,128]{2,1,0:T(8,128)} %refs_4_.1, pred[]{:T(512)S(6)} %eq.13), kind=kLoop, calls=%fused_computation.10 | loop fusion | flops 81920 | bytes 655361 | tf_op jit(solution)/shard_map/jit(_where)/select_n | solution.py:528
  1.7 3.0 %collective-permute-start.1 = (f32[10,32,128]{2,1,0:T(8,128)S(1)}, f32[10,32,128]{2,1,0:T(8,128)S(1)}, u32[]{:S(2)}, u32[]{:S(2)}) collective-permute-start(f32[10,32,128]{2,1,0:T(8,128)S(1)} %get-tuple-element.67), channel_id=1, source_target_pairs={{0,4},{8,12},{16,20},{24,28},{4,0},{12,8},{20,16},{28,24},{1,5},{9... | collective-permute-start | bytes 491528 | tf_op jit(solution)/shard_map/ppermute | solution.py:530
  4.8 0.7 collective-permute-start
  5.4 0.0 copy-done
  5.5 6.3 %collective-permute-done.1 = f32[10,32,128]{2,1,0:T(8,128)S(1)} collective-permute-done((f32[10,32,128]{2,1,0:T(8,128)S(1)}, f32[10,32,128]{2,1,0:T(8,128)S(1)}, u32[]{:S(2)}, u32[]{:S(2)}) %collective-permute-start.1) | collective-permute-done | bytes 163872 | tf_op jit(solution)/shard_map/ppermute | solution.py:530
  11.8 0.0 collective-permute-done
  11.9 0.7 collective-permute-start.2
  12.6 2.9 %collective-permute-start.3 = (f32[360,128]{1,0:T(8,128)S(1)}, f32[360,128]{1,0:T(8,128)S(1)}, u32[]{:S(2)}, u32[]{:S(2)}) collective-permute-start(f32[360,128]{1,0:T(8,128)S(1)} %select_n.113), channel_id=1, source_target_pairs={{0,1},{2,3},{1,0},{3,2},{4,5},{6,7},{5,4},{7,6},{8,9},{10,11},{9,8... | collective-permute-start | bytes 552968 | tf_op jit(solution)/shard_map/ppermute | solution.py:530
  15.6 0.0 collective-permute-done.2
  15.6 1.1 %collective-permute-done.3 = f32[360,128]{1,0:T(8,128)S(1)} collective-permute-done((f32[360,128]{1,0:T(8,128)S(1)}, f32[360,128]{1,0:T(8,128)S(1)}, u32[]{:S(2)}, u32[]{:S(2)}) %collective-permute-start.3) | collective-permute-done | bytes 184352 | tf_op jit(solution)/shard_map/ppermute | solution.py:530
  16.6 0.0 copy-start.2
  16.7 0.0 copy-start.3
  16.7 0.7 copy-done.2
  17.3 0.0 copy-done.3
  17.3 4.4 %down.1 = (f32[20,36,128]{2,1,0:T(8,128)S(1)}, f32[20,36,128]{2,1,0:T(8,128)S(1)}, f32[16,24,128]{2,1,0:T(8,128)S(1)}, f32[16,24,128]{2,1,0:T(8,128)S(1)}, f32[4,8,128]{2,1,0:T(8,128)S(1)}) custom-call(f32[9,27]{1,0:T(8,128)S(1)} %copy-done.2, s32[6]{0:T(128)S(1)} %copy-done.3, s32[1]{0:T(128)} %constant.29.clone.1.refs_2_, ...), custom_call_target="tpu_custom_call" | custom-call | tf_op jit(solution)/shard_map/down/pallas_call | solution.py:513
  21.8 0.0 copy-start.1
  21.8 18.5 %all_to_all.15.refs_3_ = f32[16,4,8,128]{3,2,1,0:T(8,128)S(1)} all-to-all(f32[16,4,8,128]{3,2,1,0:T(8,128)S(1)} %broadcast_in_dim.8), channel_id=1, replica_groups=mesh['gx'=8,'y'=2,'core'=2] {'gx','y'}, dimensions={0} | all-to-all | bytes 524288 | tf_op jit(solution)/shard_map/all_to_all | solution.py:556
  40.3 0.0 collective-permute-start.4
  40.3 1.5 %collective-permute-done.4.refs_4_ = f32[16,4,8,128]{3,2,1,0:T(8,128)S(1)} collective-permute-done((f32[16,4,8,128]{3,2,1,0:T(8,128)S(1)}, f32[16,4,8,128]{3,2,1,0:T(8,128)S(1)}, u32[]{:S(2)}, u32[]{:S(2)}) %collective-permute-start.4) | collective-permute-done | bytes 262176 | tf_op jit(solution)/shard_map/ppermute | solution.py:559
  41.8 0.0 copy-done.1
  41.8 7.1 %up.1 = (f32[16,32,128]{2,1,0:T(8,128)}, f32[16,32,128]{2,1,0:T(8,128)S(1)}, f32[20,36,128]{2,1,0:T(8,128)S(1)}, f32[16,24,128]{2,1,0:T(8,128)S(1)}, f32[6,48,12...) custom-call(f32[9,27]{1,0:T(8,128)S(1)} %copy-done.2, ...), custom_call_target="tpu_custom_call" | custom-call | tf_op jit(solution)/shard_map/up/pallas_call | solution.py:513
  49.0 1.0 collective-permute-start.6
  49.9 0.7 collective-permute-start.5
  50.6 4.6 %collective-permute-done.6 = f32[10,32,128]{2,1,0:T(8,128)S(1)} collective-permute-done((f32[10,32,128]{2,1,0:T(8,128)S(1)}, f32[10,32,128]{2,1,0:T(8,128)S(1)}, u32[]{:S(2)}, u32[]{:S(2)}) %collective-permute-start.6) | collective-permute-done | bytes 163872 | tf_op jit(solution)/shard_map/ppermute | solution.py:530
  55.3 0.0 collective-permute-done.5
  55.5 0.7 collective-permute-start.7
  56.1 2.4 %collective-permute-start.8 = (f32[360,128]{1,0:T(8,128)S(1)}, f32[360,128]{1,0:T(8,128)S(1)}, u32[]{:S(2)}, u32[]{:S(2)}) collective-permute-start(f32[360,128]{1,0:T(8,128)S(1)} %select_n.123), channel_id=1, source_target_pairs={{0,1},{2,3},{1,0},{3,2},{4,5},{6,7},{5,4},{7,6},{8,9},{10,11},{9,8... | collective-permute-start | bytes 552968 | tf_op jit(solution)/shard_map/ppermute | solution.py:530
  58.5 0.0 collective-permute-done.7
  58.5 1.1 %collective-permute-done.8 = f32[360,128]{1,0:T(8,128)S(1)} collective-permute-done((f32[360,128]{1,0:T(8,128)S(1)}, f32[360,128]{1,0:T(8,128)S(1)}, u32[]{:S(2)}, u32[]{:S(2)}) %collective-permute-start.8) | collective-permute-done | bytes 184352 | tf_op jit(solution)/shard_map/ppermute | solution.py:530
  59.6 4.5 %down_back.1 = (f32[20,36,128]{2,1,0:T(8,128)S(1)}, f32[20,36,128]{2,1,0:T(8,128)S(1)}, f32[16,24,128]{2,1,0:T(8,128)S(1)}, f32[16,24,128]{2,1,0:T(8,128)S(1)}, f32[4,8,128]{2,1,0:T(8,128)S(1)}) custom-call(f32[9,27]{1,0:T(8,128)S(1)} %copy-done.2, s32[6]{0:T(128)S(1)} %copy-done.3, s32[1]{0:T(128)} %constant.29.clone.1.refs_2_, ...), custom_call_target="tpu_custom_call" | custom-call | tf_op jit(solution)/shard_map/down_back/pallas_call | solution.py:513
  64.1 18.3 %all_to_all.16.refs_3_ = f32[16,4,8,128]{3,2,1,0:T(8,128)S(1)} all-to-all(f32[16,4,8,128]{3,2,1,0:T(8,128)S(1)} %broadcast_in_dim.9), channel_id=1, replica_groups=mesh['gx'=8,'y'=2,'core'=2] {'gx','y'}, dimensions={0} | all-to-all | bytes 524288 | tf_op jit(solution)/shard_map/all_to_all | solution.py:556
  82.4 0.0 collective-permute-start.9
  82.4 1.5 %collective-permute-done.9.refs_4_ = f32[16,4,8,128]{3,2,1,0:T(8,128)S(1)} collective-permute-done((f32[16,4,8,128]{3,2,1,0:T(8,128)S(1)}, f32[16,4,8,128]{3,2,1,0:T(8,128)S(1)}, u32[]{:S(2)}, u32[]{:S(2)}) %collective-permute-start.9) | collective-permute-done | bytes 262176 | tf_op jit(solution)/shard_map/ppermute | solution.py:559
  83.9 8.9 %up_back.1 = (f32[16,32,128]{2,1,0:T(8,128)}, f32[1,288]{1,0:T(1,128)S(1)}) custom-call(f32[9,27]{1,0:T(8,128)S(1)} %copy-done.2, s32[6]{0:T(128)S(1)} %copy-done.3, s32[1]{0:T(128)} %constant.29.clone.1.refs_2_, f32[16,4,8,128]{3,2,1,0:T(8,128)S(1)} %all_to_all.16.refs_3_, f32[16,4,8,128]{3,2,1,0:T(8,128)S(1)} %collective-permute-done.9.refs_4_, ...), custom_call_target="tpu_custom_call" | custom-call | tf_op jit(solution)/shard_map/up_back/pallas_call | solution.py:513
  92.8 9.7 %all_to_all.17.found = f32[32,1,288]{2,1,0:T(1,128)S(1)} all-to-all(f32[32,1,288]{2,1,0:T(1,128)S(1)} %broadcast_in_dim.11), channel_id=1, replica_groups=mesh['gx'=8,'y'=2,'core'=2] {'gx','y','core'}, dimensions={0} | all-to-all | bytes 73728 | tf_op jit(solution)/shard_map/all_to_all | solution.py:550
  102.5 0.7 final.1
  (20 shorter events, 0.5 us)
Async XLA Ops:
  0.6 4.8 %copy-start = (f32[16,32,128]{2,1,0:T(8,128)S(1)}, f32[16,32,128]{2,1,0:T(8,128)}, u32[]{:S(2)}) copy-start(f32[16,32,128]{2,1,0:T(8,128)} %refs_4_.1) | copy-start | bytes 786436
  1.7 10.0 %collective-permute-start.1 = (f32[10,32,128]{2,1,0:T(8,128)S(1)}, f32[10,32,128]{2,1,0:T(8,128)S(1)}, u32[]{:S(2)}, u32[]{:S(2)}) collective-permute-start(f32[10,32,128]{2,1,0:T(8,128)S(1)} %get-tuple-element.67), channel_id=1, source_target_pairs={{0,4},{8,12},{16,20},{24,28},{4,0},{12,8},{20,16},{28,24},{1,5},{9... | collective-permute-start | bytes 491528 | tf_op jit(solution)/shard_map/ppermute | solution.py:530
  4.8 7.0 %collective-permute-start = (f32[10,32,128]{2,1,0:T(8,128)S(1)}, f32[10,32,128]{2,1,0:T(8,128)S(1)}, u32[]{:S(2)}, u32[]{:S(2)}) collective-permute-start(f32[10,32,128]{2,1,0:T(8,128)S(1)} %get-tuple-element.68), channel_id=1, source_target_pairs={{4,8},{12,16},{20,24},{8,4},{16,12},{24,20},{5,9},{13,17},{21,25},... | collective-permute-start | bytes 491528 | tf_op jit(solution)/shard_map/ppermute | solution.py:530
  11.9 3.6 %collective-permute-start.2 = (f32[360,128]{1,0:T(8,128)S(1)}, f32[360,128]{1,0:T(8,128)S(1)}, u32[]{:S(2)}, u32[]{:S(2)}) collective-permute-start(f32[360,128]{1,0:T(8,128)S(1)} %select_n.111), channel_id=1, source_target_pairs={{1,2},{2,1},{5,6},{6,5},{9,10},{10,9},{13,14},{14,13},{17,18},{18,... | collective-permute-start | bytes 552968 | tf_op jit(solution)/shard_map/ppermute | solution.py:530
  12.6 4.0 %collective-permute-start.3 = (f32[360,128]{1,0:T(8,128)S(1)}, f32[360,128]{1,0:T(8,128)S(1)}, u32[]{:S(2)}, u32[]{:S(2)}) collective-permute-start(f32[360,128]{1,0:T(8,128)S(1)} %select_n.113), channel_id=1, source_target_pairs={{0,1},{2,3},{1,0},{3,2},{4,5},{6,7},{5,4},{7,6},{8,9},{10,11},{9,8... | collective-permute-start | bytes 552968 | tf_op jit(solution)/shard_map/ppermute | solution.py:530
  16.6 0.7 copy-start.2
  16.7 0.7 copy-start.3
  21.8 20.0 %copy-start.1 = (f32[16,32,128]{2,1,0:T(8,128)S(1)}, f32[16,32,128]{2,1,0:T(8,128)}, u32[]{:S(2)}) copy-start(f32[16,32,128]{2,1,0:T(8,128)} %refs_9_.1) | copy-start | bytes 786436
  40.3 1.5 %collective-permute-start.4 = (f32[16,4,8,128]{3,2,1,0:T(8,128)S(1)}, f32[16,4,8,128]{3,2,1,0:T(8,128)S(1)}, u32[]{:S(2)}, u32[]{:S(2)}) collective-permute-start(f32[16,4,8,128]{3,2,1,0:T(8,128)S(1)} %all_to_all.15.refs_3_), channel_id=1, source_target_pairs={{0,1},{1,0},{2,3},{3,2},{4,5},{5,4},{6,7},{7,6},{8,9},{9,8},{10,11... | collective-permute-start | bytes 786440 | tf_op jit(solution)/shard_map/ppermute | solution.py:559
  49.0 6.3 %collective-permute-start.6 = (f32[10,32,128]{2,1,0:T(8,128)S(1)}, f32[10,32,128]{2,1,0:T(8,128)S(1)}, u32[]{:S(2)}, u32[]{:S(2)}) collective-permute-start(f32[10,32,128]{2,1,0:T(8,128)S(1)} %get-tuple-element.63), channel_id=1, source_target_pairs={{0,4},{8,12},{16,20},{24,28},{4,0},{12,8},{20,16},{28,24},{1,5},{9... | collective-permute-start | bytes 491528 | tf_op jit(solution)/shard_map/ppermute | solution.py:530
  49.9 5.3 %collective-permute-start.5 = (f32[10,32,128]{2,1,0:T(8,128)S(1)}, f32[10,32,128]{2,1,0:T(8,128)S(1)}, u32[]{:S(2)}, u32[]{:S(2)}) collective-permute-start(f32[10,32,128]{2,1,0:T(8,128)S(1)} %get-tuple-element.64), channel_id=1, source_target_pairs={{4,8},{12,16},{20,24},{8,4},{16,12},{24,20},{5,9},{13,17},{21,25},... | collective-permute-start | bytes 491528 | tf_op jit(solution)/shard_map/ppermute | solution.py:530
  55.5 3.1 %collective-permute-start.7 = (f32[360,128]{1,0:T(8,128)S(1)}, f32[360,128]{1,0:T(8,128)S(1)}, u32[]{:S(2)}, u32[]{:S(2)}) collective-permute-start(f32[360,128]{1,0:T(8,128)S(1)} %select_n.121), channel_id=1, source_target_pairs={{1,2},{2,1},{5,6},{6,5},{9,10},{10,9},{13,14},{14,13},{17,18},{18,... | collective-permute-start | bytes 552968 | tf_op jit(solution)/shard_map/ppermute | solution.py:530
  56.1 3.4 %collective-permute-start.8 = (f32[360,128]{1,0:T(8,128)S(1)}, f32[360,128]{1,0:T(8,128)S(1)}, u32[]{:S(2)}, u32[]{:S(2)}) collective-permute-start(f32[360,128]{1,0:T(8,128)S(1)} %select_n.123), channel_id=1, source_target_pairs={{0,1},{2,3},{1,0},{3,2},{4,5},{6,7},{5,4},{7,6},{8,9},{10,11},{9,8... | collective-permute-start | bytes 552968 | tf_op jit(solution)/shard_map/ppermute | solution.py:530
  82.4 1.5 %collective-permute-start.9 = (f32[16,4,8,128]{3,2,1,0:T(8,128)S(1)}, f32[16,4,8,128]{3,2,1,0:T(8,128)S(1)}, u32[]{:S(2)}, u32[]{:S(2)}) collective-permute-start(f32[16,4,8,128]{3,2,1,0:T(8,128)S(1)} %all_to_all.16.refs_3_), channel_id=1, source_target_pairs={{0,1},{1,0},{2,3},{3,2},{4,5},{5,4},{6,7},{7,6},{8,9},{9,8},{10,11... | collective-permute-start | bytes 786440 | tf_op jit(solution)/shard_map/ppermute | solution.py:559
